TPU v7x, 256 devices: a whole 4x4x8 slice. The times are simulated.
256 devices in a mesh: row: 16 (over z, core), col: 16 (over x, y).
Axes of the slice: x: 4, y: 4, z: 8, core: 2. Of those that a mesh axis runs over, the one named last changes fastest.
Arguments:
- right_side: float32 [1, 16, 4, 1024], P(None, 'row'), may hold values from -6 to 6
- inverse_t: bfloat16 [1, 16, 1024, 1024], P(None, 'row', 'col'), as said below
- u_factor: bfloat16 [1, 16, 1, 16, 128, 1024], P(None, 'row', None, 'col'), may hold values from -0.25 to 0.25
- v_factor: bfloat16 [1, 16, 1, 16, 128, 1024], P(None, 'row', None, 'col'), may hold values from -0.1875 to 0.1875
- ranks: int32 [1, 16, 1, 16], P(None, 'row', None, 'col'), may hold values from 4 to 128, as said below
Outputs:
- whitened: float32 [1, 16, 4, 1024], P(None, 'row')
- loglik: float32 [1, 16, 4], P(None, 'row')
Inputs may be any that keep to these rules, and one draw needn't show every extreme that they name: Tile (i, j) with j < i uses the first ranks of its factor rows. `inverse_t`: upper triangular with a positive diagonal.
All inputs are finite; a program needn't handle non-finite values.
Results may differ from a plain program's by a relative error of at most 0.0085.
Values sent between devices are 32-bit elements; how exact they have to be, the bound alone decides.
A program may use at most 64 MiB of HBM per device.

v0:
```python
import functools
import math

import jax
import jax.numpy as jnp
from jax import lax
from jax.sharding import Mesh
from jax.sharding import PartitionSpec as P

ROW = ("row_0", "row_1")
COL = ("col_0", "col_1")


def cut_along(array, dim, devices):
    lengths = array.shape
    pieces = array.reshape(*lengths[:dim], devices, lengths[dim] // devices, *lengths[dim + 1 :])
    return jnp.moveaxis(pieces, dim, 0)


def summed_on_arrival(array, axis, dim):
    pieces = cut_along(array, dim, lax.axis_size(axis))
    arrived = lax.all_to_all(pieces, axis, split_axis=0, concat_axis=0, tiled=True)
    return arrived.sum(axis=0)


def from_everyone(array, axis):
    devices = lax.axis_size(axis)
    return lax.all_to_all(
        jnp.broadcast_to(array[None], (devices, *array.shape)), axis, 0, 0, tiled=True
    )


def taken_together(array, axis):
    return from_everyone(array, axis).sum(axis=0)


def over_axes(array, axes):
    far, near = axes
    return taken_together(taken_together(array, near), far)


def one_axis_at_a_time(array, axes):
    return functools.reduce(lax.psum, axes, array)


def rank_part(v_tiles, u_tiles, rounded, limit, offset):
    width = v_tiles.shape[1]
    inner = jnp.einsum("brn,bkn->brk", v_tiles, rounded, preferred_element_type=jnp.float32)
    keep = jnp.arange(width, dtype=jnp.int32)[None, :] + offset < limit[:, None]
    inner = jnp.where(keep[:, :, None], inner, 0.0).astype(jnp.bfloat16)
    return jnp.einsum("brk,brn->bkn", inner, u_tiles, preferred_element_type=jnp.float32)


def project(v_tiles, u_tiles, rounded, limit):
    half = v_tiles.shape[1] // 2
    lower = rank_part(v_tiles[:, :half], u_tiles[:, :half], rounded, limit, 0)
    empty = jnp.zeros(lower.shape, jnp.float32)
    upper = lax.cond(
        jnp.any(limit > half),
        lambda: rank_part(v_tiles[:, half:], u_tiles[:, half:], rounded, limit, half),
        lambda: empty,
    )
    return lower + upper


def local(right_side, inverse_t, u_factor, v_factor, ranks):
    n_row = lax.axis_size(ROW)
    n_col = lax.axis_size(COL)
    cycles = right_side.shape[0]
    nrhs = right_side.shape[2]
    width = right_side.shape[3]
    slab = cycles * n_row
    per_col = slab // n_col
    piece = width // n_col
    rank_max = u_factor.shape[4]
    my_row = lax.axis_index(ROW)
    my_col = lax.axis_index(COL)
    sources = right_side.reshape(cycles, nrhs, width)
    inverse = inverse_t.reshape(cycles, piece, width)
    u_tiles = u_factor.reshape(cycles, per_col, rank_max, width)
    v_tiles = v_factor.reshape(cycles, per_col, rank_max, width)
    limits = ranks.reshape(cycles, per_col)
    block_start = my_col * piece

    def finish(partial_value, cycle, index):
        summed = summed_on_arrival(partial_value, COL, 1)
        own_source = lax.dynamic_index_in_dim(sources, cycle, 0, False)
        local_source = lax.dynamic_slice_in_dim(own_source, block_start, piece, 1)
        reduced = (local_source - summed).astype(jnp.bfloat16)
        term = jnp.dot(
            reduced,
            lax.dynamic_index_in_dim(inverse, cycle, 0, False),
            preferred_element_type=jnp.float32,
        )
        owner = index % n_row == my_row
        term = jnp.where(owner, term, 0.0)
        return over_axes(term, ("row_0", ("row_1", "col_0", "col_1")))

    empty_rows = jnp.zeros((slab, nrhs, width), jnp.float32)

    def right_step(index, carry):
        solved, pending = carry
        cycle = index // n_row
        result = finish(lax.dynamic_index_in_dim(pending, cycle, 0, False), cycle, index)
        solved = lax.dynamic_update_index_in_dim(solved, result, index, 0)
        tile_col = index // n_col
        active = index % n_col == my_col
        later = jnp.arange(cycles, dtype=jnp.int32) * n_row + my_row > index
        column_limit = lax.dynamic_index_in_dim(limits, tile_col, 1, False)
        limit = jnp.where(later & active, column_limit, 0)
        v_column = lax.dynamic_index_in_dim(v_tiles, tile_col, 1, False)
        u_column = lax.dynamic_index_in_dim(u_tiles, tile_col, 1, False)
        rounded = result.astype(jnp.bfloat16)[None]
        pending = pending + project(v_column, u_column, rounded, limit)
        return (solved, pending)

    solved, pending = lax.fori_loop(
        0, slab, right_step, (empty_rows, jnp.zeros((cycles, nrhs, width), jnp.float32))
    )
    square_block = lax.dynamic_slice_in_dim(inverse, block_start, piece, 2)
    diagonal = jnp.diagonal(square_block, axis1=1, axis2=2).astype(jnp.float32)
    log_sums = jnp.sum(jnp.log(diagonal), axis=1)
    logdiag = one_axis_at_a_time(log_sums, COL) / width
    own_rows = lax.dynamic_index_in_dim(solved.reshape(cycles, n_row, nrhs, width), my_row, 1, True)
    quadratic = jnp.mean(own_rows * own_rows, axis=3)
    loglik = -0.5 * quadratic + logdiag[:, None, None] - 0.5 * math.log(2.0 * math.pi)
    return (own_rows, loglik)


def solution(mesh):
    torus = Mesh(mesh.devices.reshape(8, 2, 4, 4), ("row_0", "row_1", "col_0", "col_1"))
    return jax.shard_map(
        local,
        mesh=torus,
        in_specs=(
            P(None, ROW, None, None),
            P(None, ROW, COL, None),
            P(None, ROW, None, COL, None, None),
            P(None, ROW, None, COL, None, None),
            P(None, ROW, None, COL),
        ),
        out_specs=(P(None, ROW, None, None), P(None, ROW, None)),
        check_vma=False,
    )
```

profile of v0, /device:TPU:225, one launch (start us, length us, event | category | flops | bytes accessed | tf_op | source)
XLA Modules:
  0.0 704.5 jit_solution(5286780681341844830)
XLA Ops:
  1.4 682.7 %while.18 = (s32[]{:T(128)}, f32[16,4,1024]{2,1,0:T(4,128)S(1)}, f32[1,4,1024]{2,1,0:T(4,128)S(1)}, s32[]{:T(128)}, f32[1,4,64]{2,1,0:T(4,128)S(1)}, /*index=5*/...) while((s32[]{:T(128)}, f32[16,4,1024]{2,1,0:T(4,128)S(1)}, ...), condition=%wide.region_6.7_spmd.clone, body=%wide.region_0.6_spmd.clone.sunk | while | flops 2807248 | bytes 6509195 | solution.py:117
  2.2 6.8 all-to-all-start
  9.0 6.4 all-to-all-done
  17.0 16.1 %all_to_all.42 = f32[32,4,1024]{2,1,0:T(4,128)S(1)} all-to-all(f32[32,4,1024]{2,1,0:T(4,128)S(1)} %broadcast_in_dim.150), channel_id=1, replica_groups=mesh['row_0'=8,'row_1'=2,'col_0'=4,'col_1'=4] {'row_1','col_0','col_1'}, dimensions={0} | all-to-all | bytes 1048576 | tf_op jit(solution)/shard_map/while/body/eval_jaxpr/all_to_all | solution.py:28
  49.2 6.4 all-to-all-done
  57.3 18.0 %all_to_all.42 = f32[32,4,1024]{2,1,0:T(4,128)S(1)} all-to-all(f32[32,4,1024]{2,1,0:T(4,128)S(1)} %broadcast_in_dim.150), channel_id=1, replica_groups=mesh['row_0'=8,'row_1'=2,'col_0'=4,'col_1'=4] {'row_1','col_0','col_1'}, dimensions={0} | all-to-all | bytes 1048576 | tf_op jit(solution)/shard_map/while/body/eval_jaxpr/all_to_all | solution.py:28
  92.0 6.4 all-to-all-done
  100.1 17.6 %all_to_all.42 = f32[32,4,1024]{2,1,0:T(4,128)S(1)} all-to-all(f32[32,4,1024]{2,1,0:T(4,128)S(1)} %broadcast_in_dim.150), channel_id=1, replica_groups=mesh['row_0'=8,'row_1'=2,'col_0'=4,'col_1'=4] {'row_1','col_0','col_1'}, dimensions={0} | all-to-all | bytes 1048576 | tf_op jit(solution)/shard_map/while/body/eval_jaxpr/all_to_all | solution.py:28
  118.4 6.3 all-to-all-start.2
  134.7 6.4 all-to-all-done
  142.7 17.6 %all_to_all.42 = f32[32,4,1024]{2,1,0:T(4,128)S(1)} all-to-all(f32[32,4,1024]{2,1,0:T(4,128)S(1)} %broadcast_in_dim.150), channel_id=1, replica_groups=mesh['row_0'=8,'row_1'=2,'col_0'=4,'col_1'=4] {'row_1','col_0','col_1'}, dimensions={0} | all-to-all | bytes 1048576 | tf_op jit(solution)/shard_map/while/body/eval_jaxpr/all_to_all | solution.py:28
  161.0 6.3 all-to-all-start.2
  177.3 6.4 all-to-all-done
  185.3 17.6 %all_to_all.42 = f32[32,4,1024]{2,1,0:T(4,128)S(1)} all-to-all(f32[32,4,1024]{2,1,0:T(4,128)S(1)} %broadcast_in_dim.150), channel_id=1, replica_groups=mesh['row_0'=8,'row_1'=2,'col_0'=4,'col_1'=4] {'row_1','col_0','col_1'}, dimensions={0} | all-to-all | bytes 1048576 | tf_op jit(solution)/shard_map/while/body/eval_jaxpr/all_to_all | solution.py:28
  219.9 6.4 all-to-all-done
  228.0 17.6 %all_to_all.42 = f32[32,4,1024]{2,1,0:T(4,128)S(1)} all-to-all(f32[32,4,1024]{2,1,0:T(4,128)S(1)} %broadcast_in_dim.150), channel_id=1, replica_groups=mesh['row_0'=8,'row_1'=2,'col_0'=4,'col_1'=4] {'row_1','col_0','col_1'}, dimensions={0} | all-to-all | bytes 1048576 | tf_op jit(solution)/shard_map/while/body/eval_jaxpr/all_to_all | solution.py:28
  246.3 6.3 all-to-all-start.2
  262.6 6.4 all-to-all-done
  270.6 17.6 %all_to_all.42 = f32[32,4,1024]{2,1,0:T(4,128)S(1)} all-to-all(f32[32,4,1024]{2,1,0:T(4,128)S(1)} %broadcast_in_dim.150), channel_id=1, replica_groups=mesh['row_0'=8,'row_1'=2,'col_0'=4,'col_1'=4] {'row_1','col_0','col_1'}, dimensions={0} | all-to-all | bytes 1048576 | tf_op jit(solution)/shard_map/while/body/eval_jaxpr/all_to_all | solution.py:28
  288.9 6.3 all-to-all-start.2
  305.2 6.4 all-to-all-done
  313.2 17.6 %all_to_all.42 = f32[32,4,1024]{2,1,0:T(4,128)S(1)} all-to-all(f32[32,4,1024]{2,1,0:T(4,128)S(1)} %broadcast_in_dim.150), channel_id=1, replica_groups=mesh['row_0'=8,'row_1'=2,'col_0'=4,'col_1'=4] {'row_1','col_0','col_1'}, dimensions={0} | all-to-all | bytes 1048576 | tf_op jit(solution)/shard_map/while/body/eval_jaxpr/all_to_all | solution.py:28
  331.5 6.3 all-to-all-start.2
  347.8 6.4 all-to-all-done
  355.8 17.6 %all_to_all.42 = f32[32,4,1024]{2,1,0:T(4,128)S(1)} all-to-all(f32[32,4,1024]{2,1,0:T(4,128)S(1)} %broadcast_in_dim.150), channel_id=1, replica_groups=mesh['row_0'=8,'row_1'=2,'col_0'=4,'col_1'=4] {'row_1','col_0','col_1'}, dimensions={0} | all-to-all | bytes 1048576 | tf_op jit(solution)/shard_map/while/body/eval_jaxpr/all_to_all | solution.py:28
  390.4 6.4 all-to-all-done
  398.5 17.6 %all_to_all.42 = f32[32,4,1024]{2,1,0:T(4,128)S(1)} all-to-all(f32[32,4,1024]{2,1,0:T(4,128)S(1)} %broadcast_in_dim.150), channel_id=1, replica_groups=mesh['row_0'=8,'row_1'=2,'col_0'=4,'col_1'=4] {'row_1','col_0','col_1'}, dimensions={0} | all-to-all | bytes 1048576 | tf_op jit(solution)/shard_map/while/body/eval_jaxpr/all_to_all | solution.py:28
  416.8 6.3 all-to-all-start.2
  433.1 6.4 all-to-all-done
  441.1 17.6 %all_to_all.42 = f32[32,4,1024]{2,1,0:T(4,128)S(1)} all-to-all(f32[32,4,1024]{2,1,0:T(4,128)S(1)} %broadcast_in_dim.150), channel_id=1, replica_groups=mesh['row_0'=8,'row_1'=2,'col_0'=4,'col_1'=4] {'row_1','col_0','col_1'}, dimensions={0} | all-to-all | bytes 1048576 | tf_op jit(solution)/shard_map/while/body/eval_jaxpr/all_to_all | solution.py:28
  459.4 6.3 all-to-all-start.2
  475.7 6.4 all-to-all-done
  483.7 17.6 %all_to_all.42 = f32[32,4,1024]{2,1,0:T(4,128)S(1)} all-to-all(f32[32,4,1024]{2,1,0:T(4,128)S(1)} %broadcast_in_dim.150), channel_id=1, replica_groups=mesh['row_0'=8,'row_1'=2,'col_0'=4,'col_1'=4] {'row_1','col_0','col_1'}, dimensions={0} | all-to-all | bytes 1048576 | tf_op jit(solution)/shard_map/while/body/eval_jaxpr/all_to_all | solution.py:28
  502.0 6.3 all-to-all-start.2
  518.3 6.4 all-to-all-done
  526.3 17.6 %all_to_all.42 = f32[32,4,1024]{2,1,0:T(4,128)S(1)} all-to-all(f32[32,4,1024]{2,1,0:T(4,128)S(1)} %broadcast_in_dim.150), channel_id=1, replica_groups=mesh['row_0'=8,'row_1'=2,'col_0'=4,'col_1'=4] {'row_1','col_0','col_1'}, dimensions={0} | all-to-all | bytes 1048576 | tf_op jit(solution)/shard_map/while/body/eval_jaxpr/all_to_all | solution.py:28
  544.7 6.3 all-to-all-start.2
  561.0 6.4 all-to-all-done
  569.0 17.6 %all_to_all.42 = f32[32,4,1024]{2,1,0:T(4,128)S(1)} all-to-all(f32[32,4,1024]{2,1,0:T(4,128)S(1)} %broadcast_in_dim.150), channel_id=1, replica_groups=mesh['row_0'=8,'row_1'=2,'col_0'=4,'col_1'=4] {'row_1','col_0','col_1'}, dimensions={0} | all-to-all | bytes 1048576 | tf_op jit(solution)/shard_map/while/body/eval_jaxpr/all_to_all | solution.py:28
  587.3 6.3 all-to-all-start.2
  603.6 6.4 all-to-all-done
  611.6 17.6 %all_to_all.42 = f32[32,4,1024]{2,1,0:T(4,128)S(1)} all-to-all(f32[32,4,1024]{2,1,0:T(4,128)S(1)} %broadcast_in_dim.150), channel_id=1, replica_groups=mesh['row_0'=8,'row_1'=2,'col_0'=4,'col_1'=4] {'row_1','col_0','col_1'}, dimensions={0} | all-to-all | bytes 1048576 | tf_op jit(solution)/shard_map/while/body/eval_jaxpr/all_to_all | solution.py:28
  629.9 6.3 all-to-all-start.2
  646.2 6.4 all-to-all-done
  654.2 17.6 %all_to_all.42 = f32[32,4,1024]{2,1,0:T(4,128)S(1)} all-to-all(f32[32,4,1024]{2,1,0:T(4,128)S(1)} %broadcast_in_dim.150), channel_id=1, replica_groups=mesh['row_0'=8,'row_1'=2,'col_0'=4,'col_1'=4] {'row_1','col_0','col_1'}, dimensions={0} | all-to-all | bytes 1048576 | tf_op jit(solution)/shard_map/while/body/eval_jaxpr/all_to_all | solution.py:28
  672.5 6.3 all-to-all-start.2
  687.2 8.3 %psum.14 = f32[1]{0:T(128)} all-reduce(f32[1]{0:T(128)} %bitcast.13), channel_id=1, replica_groups=mesh['row_0'=8,'row_1'=2,'col_0'=4,'col_1'=4] {'col_0'}, use_global_device_ids=true, to_apply=%region_9.10 | all-reduce | flops 1 | bytes 8 | tf_op jit(solution)/shard_map/psum | solution.py:43
  695.4 7.9 %psum.15 = f32[1]{0:T(128)} all-reduce(f32[1]{0:T(128)} %psum.14), channel_id=1, replica_groups=mesh['row_0'=8,'row_1'=2,'col_0'=4,'col_1'=4] {'col_1'}, use_global_device_ids=true, to_apply=%region_10.11 | all-reduce | flops 1 | bytes 8 | tf_op jit(solution)/shard_map/psum | solution.py:43
  (430 shorter events, 209.9 us)
Async XLA Ops:
  1.5 15.3 %copy-start.3 = (bf16[1,64,1024]{2,1,0:T(8,128)(2,1)S(1)}, bf16[1,64,1024]{2,1,0:T(8,128)(2,1)}, u32[]{:S(2)}) copy-start(bf16[1,64,1024]{2,1,0:T(8,128)(2,1)} %get-tuple-element.450) | copy-start | bytes 393220 | tf_op jit(solution)/shard_map/while
  2.2 13.2 %all-to-all-start = ((f32[16,1,256]{2,1,0:T(1,128)}), f32[16,1,256]{2,1,0:T(1,128)S(1)}, u32[]{:S(2)}, u32[]{:S(2)}) async-start(f32[16,1,256]{2,1,0:T(1,128)} %reshape.227), calls=%async_computation | async-start | bytes 32768 | tf_op jit(solution)/shard_map/while/body/eval_jaxpr/all_to_all | solution.py:22
  33.9 10.3 %all-to-all-start.2 = ((f32[8,4,1024]{2,1,0:T(4,128)}), f32[8,4,1024]{2,1,0:T(4,128)S(1)}, u32[]{:S(2)}, u32[]{:S(2)}) async-start(f32[8,4,1024]{2,1,0:T(4,128)} %broadcast_in_dim.151), calls=%async_computation.2 | async-start | bytes 262144 | tf_op jit(solution)/shard_map/while/body/eval_jaxpr/all_to_all | solution.py:28
  44.7 12.3 %copy-start.3 = (bf16[1,64,1024]{2,1,0:T(8,128)(2,1)S(1)}, bf16[1,64,1024]{2,1,0:T(8,128)(2,1)}, u32[]{:S(2)}) copy-start(bf16[1,64,1024]{2,1,0:T(8,128)(2,1)} %get-tuple-element.450) | copy-start | bytes 393220 | tf_op jit(solution)/shard_map/while
  45.5 10.2 %all-to-all-start = ((f32[16,1,256]{2,1,0:T(1,128)}), f32[16,1,256]{2,1,0:T(1,128)S(1)}, u32[]{:S(2)}, u32[]{:S(2)}) async-start(f32[16,1,256]{2,1,0:T(1,128)} %reshape.227), calls=%async_computation | async-start | bytes 32768 | tf_op jit(solution)/shard_map/while/body/eval_jaxpr/all_to_all | solution.py:22
  76.0 10.9 %all-to-all-start.2 = ((f32[8,4,1024]{2,1,0:T(4,128)}), f32[8,4,1024]{2,1,0:T(4,128)S(1)}, u32[]{:S(2)}, u32[]{:S(2)}) async-start(f32[8,4,1024]{2,1,0:T(4,128)} %broadcast_in_dim.151), calls=%async_computation.2 | async-start | bytes 262144 | tf_op jit(solution)/shard_map/while/body/eval_jaxpr/all_to_all | solution.py:28
  87.5 12.3 %copy-start.3 = (bf16[1,64,1024]{2,1,0:T(8,128)(2,1)S(1)}, bf16[1,64,1024]{2,1,0:T(8,128)(2,1)}, u32[]{:S(2)}) copy-start(bf16[1,64,1024]{2,1,0:T(8,128)(2,1)} %get-tuple-element.450) | copy-start | bytes 393220 | tf_op jit(solution)/shard_map/while
  88.2 10.3 %all-to-all-start = ((f32[16,1,256]{2,1,0:T(1,128)}), f32[16,1,256]{2,1,0:T(1,128)S(1)}, u32[]{:S(2)}, u32[]{:S(2)}) async-start(f32[16,1,256]{2,1,0:T(1,128)} %reshape.227), calls=%async_computation | async-start | bytes 32768 | tf_op jit(solution)/shard_map/while/body/eval_jaxpr/all_to_all | solution.py:22
  118.4 11.2 %all-to-all-start.2 = ((f32[8,4,1024]{2,1,0:T(4,128)}), f32[8,4,1024]{2,1,0:T(4,128)S(1)}, u32[]{:S(2)}, u32[]{:S(2)}) async-start(f32[8,4,1024]{2,1,0:T(4,128)} %broadcast_in_dim.151), calls=%async_computation.2 | async-start | bytes 262144 | tf_op jit(solution)/shard_map/while/body/eval_jaxpr/all_to_all | solution.py:28
  130.1 12.3 %copy-start.3 = (bf16[1,64,1024]{2,1,0:T(8,128)(2,1)S(1)}, bf16[1,64,1024]{2,1,0:T(8,128)(2,1)}, u32[]{:S(2)}) copy-start(bf16[1,64,1024]{2,1,0:T(8,128)(2,1)} %get-tuple-element.450) | copy-start | bytes 393220 | tf_op jit(solution)/shard_map/while
  130.8 10.3 %all-to-all-start = ((f32[16,1,256]{2,1,0:T(1,128)}), f32[16,1,256]{2,1,0:T(1,128)S(1)}, u32[]{:S(2)}, u32[]{:S(2)}) async-start(f32[16,1,256]{2,1,0:T(1,128)} %reshape.227), calls=%async_computation | async-start | bytes 32768 | tf_op jit(solution)/shard_map/while/body/eval_jaxpr/all_to_all | solution.py:22
  161.0 11.2 %all-to-all-start.2 = ((f32[8,4,1024]{2,1,0:T(4,128)}), f32[8,4,1024]{2,1,0:T(4,128)S(1)}, u32[]{:S(2)}, u32[]{:S(2)}) async-start(f32[8,4,1024]{2,1,0:T(4,128)} %broadcast_in_dim.151), calls=%async_computation.2 | async-start | bytes 262144 | tf_op jit(solution)/shard_map/while/body/eval_jaxpr/all_to_all | solution.py:28
  172.7 12.3 %copy-start.3 = (bf16[1,64,1024]{2,1,0:T(8,128)(2,1)S(1)}, bf16[1,64,1024]{2,1,0:T(8,128)(2,1)}, u32[]{:S(2)}) copy-start(bf16[1,64,1024]{2,1,0:T(8,128)(2,1)} %get-tuple-element.450) | copy-start | bytes 393220 | tf_op jit(solution)/shard_map/while
  173.4 10.3 %all-to-all-start = ((f32[16,1,256]{2,1,0:T(1,128)}), f32[16,1,256]{2,1,0:T(1,128)S(1)}, u32[]{:S(2)}, u32[]{:S(2)}) async-start(f32[16,1,256]{2,1,0:T(1,128)} %reshape.227), calls=%async_computation | async-start | bytes 32768 | tf_op jit(solution)/shard_map/while/body/eval_jaxpr/all_to_all | solution.py:22
  203.6 11.2 %all-to-all-start.2 = ((f32[8,4,1024]{2,1,0:T(4,128)}), f32[8,4,1024]{2,1,0:T(4,128)S(1)}, u32[]{:S(2)}, u32[]{:S(2)}) async-start(f32[8,4,1024]{2,1,0:T(4,128)} %broadcast_in_dim.151), calls=%async_computation.2 | async-start | bytes 262144 | tf_op jit(solution)/shard_map/while/body/eval_jaxpr/all_to_all | solution.py:28
  215.3 12.3 %copy-start.3 = (bf16[1,64,1024]{2,1,0:T(8,128)(2,1)S(1)}, bf16[1,64,1024]{2,1,0:T(8,128)(2,1)}, u32[]{:S(2)}) copy-start(bf16[1,64,1024]{2,1,0:T(8,128)(2,1)} %get-tuple-element.450) | copy-start | bytes 393220 | tf_op jit(solution)/shard_map/while
  216.1 10.3 %all-to-all-start = ((f32[16,1,256]{2,1,0:T(1,128)}), f32[16,1,256]{2,1,0:T(1,128)S(1)}, u32[]{:S(2)}, u32[]{:S(2)}) async-start(f32[16,1,256]{2,1,0:T(1,128)} %reshape.227), calls=%async_computation | async-start | bytes 32768 | tf_op jit(solution)/shard_map/while/body/eval_jaxpr/all_to_all | solution.py:22
  246.3 11.2 %all-to-all-start.2 = ((f32[8,4,1024]{2,1,0:T(4,128)}), f32[8,4,1024]{2,1,0:T(4,128)S(1)}, u32[]{:S(2)}, u32[]{:S(2)}) async-start(f32[8,4,1024]{2,1,0:T(4,128)} %broadcast_in_dim.151), calls=%async_computation.2 | async-start | bytes 262144 | tf_op jit(solution)/shard_map/while/body/eval_jaxpr/all_to_all | solution.py:28
  258.0 12.3 %copy-start.3 = (bf16[1,64,1024]{2,1,0:T(8,128)(2,1)S(1)}, bf16[1,64,1024]{2,1,0:T(8,128)(2,1)}, u32[]{:S(2)}) copy-start(bf16[1,64,1024]{2,1,0:T(8,128)(2,1)} %get-tuple-element.450) | copy-start | bytes 393220 | tf_op jit(solution)/shard_map/while
  258.7 10.3 %all-to-all-start = ((f32[16,1,256]{2,1,0:T(1,128)}), f32[16,1,256]{2,1,0:T(1,128)S(1)}, u32[]{:S(2)}, u32[]{:S(2)}) async-start(f32[16,1,256]{2,1,0:T(1,128)} %reshape.227), calls=%async_computation | async-start | bytes 32768 | tf_op jit(solution)/shard_map/while/body/eval_jaxpr/all_to_all | solution.py:22
  288.9 11.2 %all-to-all-start.2 = ((f32[8,4,1024]{2,1,0:T(4,128)}), f32[8,4,1024]{2,1,0:T(4,128)S(1)}, u32[]{:S(2)}, u32[]{:S(2)}) async-start(f32[8,4,1024]{2,1,0:T(4,128)} %broadcast_in_dim.151), calls=%async_computation.2 | async-start | bytes 262144 | tf_op jit(solution)/shard_map/while/body/eval_jaxpr/all_to_all | solution.py:28
  300.6 12.3 %copy-start.3 = (bf16[1,64,1024]{2,1,0:T(8,128)(2,1)S(1)}, bf16[1,64,1024]{2,1,0:T(8,128)(2,1)}, u32[]{:S(2)}) copy-start(bf16[1,64,1024]{2,1,0:T(8,128)(2,1)} %get-tuple-element.450) | copy-start | bytes 393220 | tf_op jit(solution)/shard_map/while
  301.3 10.3 %all-to-all-start = ((f32[16,1,256]{2,1,0:T(1,128)}), f32[16,1,256]{2,1,0:T(1,128)S(1)}, u32[]{:S(2)}, u32[]{:S(2)}) async-start(f32[16,1,256]{2,1,0:T(1,128)} %reshape.227), calls=%async_computation | async-start | bytes 32768 | tf_op jit(solution)/shard_map/while/body/eval_jaxpr/all_to_all | solution.py:22
  331.5 11.2 %all-to-all-start.2 = ((f32[8,4,1024]{2,1,0:T(4,128)}), f32[8,4,1024]{2,1,0:T(4,128)S(1)}, u32[]{:S(2)}, u32[]{:S(2)}) async-start(f32[8,4,1024]{2,1,0:T(4,128)} %broadcast_in_dim.151), calls=%async_computation.2 | async-start | bytes 262144 | tf_op jit(solution)/shard_map/while/body/eval_jaxpr/all_to_all | solution.py:28
  343.2 12.3 %copy-start.3 = (bf16[1,64,1024]{2,1,0:T(8,128)(2,1)S(1)}, bf16[1,64,1024]{2,1,0:T(8,128)(2,1)}, u32[]{:S(2)}) copy-start(bf16[1,64,1024]{2,1,0:T(8,128)(2,1)} %get-tuple-element.450) | copy-start | bytes 393220 | tf_op jit(solution)/shard_map/while
  343.9 10.3 %all-to-all-start = ((f32[16,1,256]{2,1,0:T(1,128)}), f32[16,1,256]{2,1,0:T(1,128)S(1)}, u32[]{:S(2)}, u32[]{:S(2)}) async-start(f32[16,1,256]{2,1,0:T(1,128)} %reshape.227), calls=%async_computation | async-start | bytes 32768 | tf_op jit(solution)/shard_map/while/body/eval_jaxpr/all_to_all | solution.py:22
  374.2 11.2 %all-to-all-start.2 = ((f32[8,4,1024]{2,1,0:T(4,128)}), f32[8,4,1024]{2,1,0:T(4,128)S(1)}, u32[]{:S(2)}, u32[]{:S(2)}) async-start(f32[8,4,1024]{2,1,0:T(4,128)} %broadcast_in_dim.151), calls=%async_computation.2 | async-start | bytes 262144 | tf_op jit(solution)/shard_map/while/body/eval_jaxpr/all_to_all | solution.py:28
  385.9 12.3 %copy-start.3 = (bf16[1,64,1024]{2,1,0:T(8,128)(2,1)S(1)}, bf16[1,64,1024]{2,1,0:T(8,128)(2,1)}, u32[]{:S(2)}) copy-start(bf16[1,64,1024]{2,1,0:T(8,128)(2,1)} %get-tuple-element.450) | copy-start | bytes 393220 | tf_op jit(solution)/shard_map/while
  386.6 10.3 %all-to-all-start = ((f32[16,1,256]{2,1,0:T(1,128)}), f32[16,1,256]{2,1,0:T(1,128)S(1)}, u32[]{:S(2)}, u32[]{:S(2)}) async-start(f32[16,1,256]{2,1,0:T(1,128)} %reshape.227), calls=%async_computation | async-start | bytes 32768 | tf_op jit(solution)/shard_map/while/body/eval_jaxpr/all_to_all | solution.py:22
  416.8 11.2 %all-to-all-start.2 = ((f32[8,4,1024]{2,1,0:T(4,128)}), f32[8,4,1024]{2,1,0:T(4,128)S(1)}, u32[]{:S(2)}, u32[]{:S(2)}) async-start(f32[8,4,1024]{2,1,0:T(4,128)} %broadcast_in_dim.151), calls=%async_computation.2 | async-start | bytes 262144 | tf_op jit(solution)/shard_map/while/body/eval_jaxpr/all_to_all | solution.py:28
  428.5 12.3 %copy-start.3 = (bf16[1,64,1024]{2,1,0:T(8,128)(2,1)S(1)}, bf16[1,64,1024]{2,1,0:T(8,128)(2,1)}, u32[]{:S(2)}) copy-start(bf16[1,64,1024]{2,1,0:T(8,128)(2,1)} %get-tuple-element.450) | copy-start | bytes 393220 | tf_op jit(solution)/shard_map/while
  429.2 10.3 %all-to-all-start = ((f32[16,1,256]{2,1,0:T(1,128)}), f32[16,1,256]{2,1,0:T(1,128)S(1)}, u32[]{:S(2)}, u32[]{:S(2)}) async-start(f32[16,1,256]{2,1,0:T(1,128)} %reshape.227), calls=%async_computation | async-start | bytes 32768 | tf_op jit(solution)/shard_map/while/body/eval_jaxpr/all_to_all | solution.py:22
  459.4 11.2 %all-to-all-start.2 = ((f32[8,4,1024]{2,1,0:T(4,128)}), f32[8,4,1024]{2,1,0:T(4,128)S(1)}, u32[]{:S(2)}, u32[]{:S(2)}) async-start(f32[8,4,1024]{2,1,0:T(4,128)} %broadcast_in_dim.151), calls=%async_computation.2 | async-start | bytes 262144 | tf_op jit(solution)/shard_map/while/body/eval_jaxpr/all_to_all | solution.py:28
  471.1 12.3 %copy-start.3 = (bf16[1,64,1024]{2,1,0:T(8,128)(2,1)S(1)}, bf16[1,64,1024]{2,1,0:T(8,128)(2,1)}, u32[]{:S(2)}) copy-start(bf16[1,64,1024]{2,1,0:T(8,128)(2,1)} %get-tuple-element.450) | copy-start | bytes 393220 | tf_op jit(solution)/shard_map/while
  471.8 10.3 %all-to-all-start = ((f32[16,1,256]{2,1,0:T(1,128)}), f32[16,1,256]{2,1,0:T(1,128)S(1)}, u32[]{:S(2)}, u32[]{:S(2)}) async-start(f32[16,1,256]{2,1,0:T(1,128)} %reshape.227), calls=%async_computation | async-start | bytes 32768 | tf_op jit(solution)/shard_map/while/body/eval_jaxpr/all_to_all | solution.py:22
  502.0 11.2 %all-to-all-start.2 = ((f32[8,4,1024]{2,1,0:T(4,128)}), f32[8,4,1024]{2,1,0:T(4,128)S(1)}, u32[]{:S(2)}, u32[]{:S(2)}) async-start(f32[8,4,1024]{2,1,0:T(4,128)} %broadcast_in_dim.151), calls=%async_computation.2 | async-start | bytes 262144 | tf_op jit(solution)/shard_map/while/body/eval_jaxpr/all_to_all | solution.py:28
  513.7 12.3 %copy-start.3 = (bf16[1,64,1024]{2,1,0:T(8,128)(2,1)S(1)}, bf16[1,64,1024]{2,1,0:T(8,128)(2,1)}, u32[]{:S(2)}) copy-start(bf16[1,64,1024]{2,1,0:T(8,128)(2,1)} %get-tuple-element.450) | copy-start | bytes 393220 | tf_op jit(solution)/shard_map/while
  514.5 10.3 %all-to-all-start = ((f32[16,1,256]{2,1,0:T(1,128)}), f32[16,1,256]{2,1,0:T(1,128)S(1)}, u32[]{:S(2)}, u32[]{:S(2)}) async-start(f32[16,1,256]{2,1,0:T(1,128)} %reshape.227), calls=%async_computation | async-start | bytes 32768 | tf_op jit(solution)/shard_map/while/body/eval_jaxpr/all_to_all | solution.py:22
  544.7 11.2 %all-to-all-start.2 = ((f32[8,4,1024]{2,1,0:T(4,128)}), f32[8,4,1024]{2,1,0:T(4,128)S(1)}, u32[]{:S(2)}, u32[]{:S(2)}) async-start(f32[8,4,1024]{2,1,0:T(4,128)} %broadcast_in_dim.151), calls=%async_computation.2 | async-start | bytes 262144 | tf_op jit(solution)/shard_map/while/body/eval_jaxpr/all_to_all | solution.py:28
  556.4 12.3 %copy-start.3 = (bf16[1,64,1024]{2,1,0:T(8,128)(2,1)S(1)}, bf16[1,64,1024]{2,1,0:T(8,128)(2,1)}, u32[]{:S(2)}) copy-start(bf16[1,64,1024]{2,1,0:T(8,128)(2,1)} %get-tuple-element.450) | copy-start | bytes 393220 | tf_op jit(solution)/shard_map/while
  557.1 10.3 %all-to-all-start = ((f32[16,1,256]{2,1,0:T(1,128)}), f32[16,1,256]{2,1,0:T(1,128)S(1)}, u32[]{:S(2)}, u32[]{:S(2)}) async-start(f32[16,1,256]{2,1,0:T(1,128)} %reshape.227), calls=%async_computation | async-start | bytes 32768 | tf_op jit(solution)/shard_map/while/body/eval_jaxpr/all_to_all | solution.py:22
  587.3 11.2 %all-to-all-start.2 = ((f32[8,4,1024]{2,1,0:T(4,128)}), f32[8,4,1024]{2,1,0:T(4,128)S(1)}, u32[]{:S(2)}, u32[]{:S(2)}) async-start(f32[8,4,1024]{2,1,0:T(4,128)} %broadcast_in_dim.151), calls=%async_computation.2 | async-start | bytes 262144 | tf_op jit(solution)/shard_map/while/body/eval_jaxpr/all_to_all | solution.py:28
  599.0 12.3 %copy-start.3 = (bf16[1,64,1024]{2,1,0:T(8,128)(2,1)S(1)}, bf16[1,64,1024]{2,1,0:T(8,128)(2,1)}, u32[]{:S(2)}) copy-start(bf16[1,64,1024]{2,1,0:T(8,128)(2,1)} %get-tuple-element.450) | copy-start | bytes 393220 | tf_op jit(solution)/shard_map/while
  599.7 10.3 %all-to-all-start = ((f32[16,1,256]{2,1,0:T(1,128)}), f32[16,1,256]{2,1,0:T(1,128)S(1)}, u32[]{:S(2)}, u32[]{:S(2)}) async-start(f32[16,1,256]{2,1,0:T(1,128)} %reshape.227), calls=%async_computation | async-start | bytes 32768 | tf_op jit(solution)/shard_map/while/body/eval_jaxpr/all_to_all | solution.py:22
  629.9 11.2 %all-to-all-start.2 = ((f32[8,4,1024]{2,1,0:T(4,128)}), f32[8,4,1024]{2,1,0:T(4,128)S(1)}, u32[]{:S(2)}, u32[]{:S(2)}) async-start(f32[8,4,1024]{2,1,0:T(4,128)} %broadcast_in_dim.151), calls=%async_computation.2 | async-start | bytes 262144 | tf_op jit(solution)/shard_map/while/body/eval_jaxpr/all_to_all | solution.py:28
  641.6 12.3 %copy-start.3 = (bf16[1,64,1024]{2,1,0:T(8,128)(2,1)S(1)}, bf16[1,64,1024]{2,1,0:T(8,128)(2,1)}, u32[]{:S(2)}) copy-start(bf16[1,64,1024]{2,1,0:T(8,128)(2,1)} %get-tuple-element.450) | copy-start | bytes 393220 | tf_op jit(solution)/shard_map/while
  642.3 10.3 %all-to-all-start = ((f32[16,1,256]{2,1,0:T(1,128)}), f32[16,1,256]{2,1,0:T(1,128)S(1)}, u32[]{:S(2)}, u32[]{:S(2)}) async-start(f32[16,1,256]{2,1,0:T(1,128)} %reshape.227), calls=%async_computation | async-start | bytes 32768 | tf_op jit(solution)/shard_map/while/body/eval_jaxpr/all_to_all | solution.py:22
  672.5 11.2 %all-to-all-start.2 = ((f32[8,4,1024]{2,1,0:T(4,128)}), f32[8,4,1024]{2,1,0:T(4,128)S(1)}, u32[]{:S(2)}, u32[]{:S(2)}) async-start(f32[8,4,1024]{2,1,0:T(4,128)} %broadcast_in_dim.151), calls=%async_computation.2 | async-start | bytes 262144 | tf_op jit(solution)/shard_map/while/body/eval_jaxpr/all_to_all | solution.py:28
  (33 other events, 368.6 us)
where the time goes:
time: 719 us; the launch traced here: 704 us
  blocking collectives  296 us (41%)
  waiting for transfers between devices  171 us (24%)
  starting transfers between devices  164 us (23%)
  local copies, waits for them, and re-layouts  37.4 us (5%)
  other arithmetic  15.5 us (2%)
  loops' own time  12.7 us (2%)
    all_to_all x16, blocking collectives, from_everyone(): lax.all_to_all(jnp.broadcast_to(array[None], (devices, *array.shape)), ax...  280 us
    all_to_all x16, waiting for transfers between devices, summed_on_arrival(): lax.all_to_all(pieces, axis, split_axis=0, concat_axis=0, tiled=True)  103 us
    all_to_all x16, starting transfers between devices, from_everyone(): lax.all_to_all(jnp.broadcast_to(array[None], (devices, *array.shape)), ax...  99.1 us
    all_to_all x16, waiting for transfers between devices, from_everyone(): lax.all_to_all(jnp.broadcast_to(array[None], (devices, *array.shape)), ax...  67.9 us
    all_to_all x16, starting transfers between devices, summed_on_arrival(): lax.all_to_all(pieces, axis, split_axis=0, concat_axis=0, tiled=True)  64.5 us
    psum x2, blocking collectives, one_axis_at_a_time(): return functools.reduce(lax.psum, axes, array)  16.1 us
  transfers between devices with their start and end apart: 32, of which 32 were waited for; matrix products, arithmetic and copies ran while one was open for 0% of the time, Pallas kernels for 0%

commit v1 on v0

v1 whole, which is shorter than its diff:
```python
import functools
import math

import jax
import jax.numpy as jnp
from jax import lax
from jax.experimental import pallas as pl
from jax.experimental.pallas import tpu as pltpu
from jax.sharding import PartitionSpec as P

MESH = pl.DeviceIdType.MESH
LANES = 128


def kernel(n, rs_ref, inv_ref, u_ref, v_ref, rank_ref, white_ref, lik_ref,
           block, whole, arrived, own_part, parts, result, final, logs, logs_in,
           block_send, block_recv, y_send, y_recv, part_send, part_recv,
           final_send, final_recv, logs_send, logs_recv):
    row = lax.axis_index("row")
    col = lax.axis_index("col")
    piece, width = inv_ref.shape
    rank_max = u_ref.shape[0]
    solver_col = lax.rem(row + n - 1, n)
    is_solver = col == solver_col
    below = col < row

    for tile in range(width // 256):
        whole[pl.ds(tile * 256 + LANES, LANES), pl.ds(tile * 256, LANES)] = jnp.zeros((LANES, LANES), jnp.float32)

    barrier = pltpu.get_barrier_semaphore()
    for step in range(1, n):
        @pl.when(is_solver)
        def _():
            pl.semaphore_signal(barrier, inc=1, device_id=(row, lax.rem(col + step, n)), device_id_type=MESH)
        @pl.when(is_solver & (row + step < n))
        def _():
            pl.semaphore_signal(barrier, inc=1, device_id=(row + step, row), device_id_type=MESH)
    @pl.when(jnp.logical_not(is_solver))
    def _():
        pl.semaphore_signal(barrier, inc=1, device_id=(row, solver_col), device_id_type=MESH)
    @pl.when(below)
    def _():
        source_col = lax.rem(col + n - 1, n)
        pl.semaphore_signal(barrier, inc=1, device_id=(col, source_col), device_id_type=MESH)
    partners = jnp.where(is_solver, 2 * (n - 1) - row, 1) + jnp.where(below, 1, 0)
    pl.semaphore_wait(barrier, partners)

    def block_copy(owner):
        first = owner * piece // LANES * LANES
        return pltpu.make_async_remote_copy(
            src_ref=block.at[:, pl.ds(first, width - first)],
            dst_ref=whole.at[pl.ds(owner * piece, piece), pl.ds(first, width - first)],
            send_sem=block_send,
            recv_sem=block_recv.at[owner],
            device_id=(row, solver_col),
            device_id_type=MESH,
        )

    block[...] = inv_ref[...].astype(jnp.float32)
    for owner in range(n):
        @pl.when((col == owner) & jnp.logical_not(is_solver))
        def _():
            block_copy(owner).start()

    def project(y):
        inner = lax.dot_general(
            y.astype(jnp.bfloat16), v_ref[...], (((1,), (1,)), ((), ())), preferred_element_type=jnp.float32
        )
        keep = lax.broadcasted_iota(jnp.int32, inner.shape, 1) < rank_ref[0, 0]
        inner = jnp.where(keep, inner, 0.0).astype(jnp.bfloat16)
        return jnp.dot(inner, u_ref[...], preferred_element_type=jnp.float32)

    def y_copy(target):
        return pltpu.make_async_remote_copy(
            src_ref=result, dst_ref=arrived, send_sem=y_send.at[target], recv_sem=y_recv,
            device_id=(target, row), device_id_type=MESH,
        )

    def part_copy():
        return pltpu.make_async_remote_copy(
            src_ref=own_part, dst_ref=parts.at[col], send_sem=part_send, recv_sem=part_recv.at[col],
            device_id=(row, solver_col), device_id_type=MESH,
        )

    def final_copy(step):
        return pltpu.make_async_remote_copy(
            src_ref=result, dst_ref=final, send_sem=final_send.at[step], recv_sem=final_recv,
            device_id=(row, lax.rem(col + step, n)), device_id_type=MESH,
        )

    def logs_copy(step):
        return pltpu.make_async_remote_copy(
            src_ref=logs, dst_ref=logs_in, send_sem=logs_send.at[step], recv_sem=logs_recv,
            device_id=(row, lax.rem(col + step, n)), device_id_type=MESH,
        )

    def finish(y, log_mean):
        quadratic = jnp.sum(y * y, axis=1, keepdims=True) * (1.0 / width)
        lik_ref[...] = -0.5 * quadratic + log_mean - 0.5 * math.log(2.0 * math.pi)
        white_ref[...] = y

    @pl.when(is_solver)
    def _():
        whole[pl.ds(pl.multiple_of(col * piece, piece), piece), :] = block[...]
        for owner in range(n):
            @pl.when(col != owner)
            def _():
                block_copy(owner).wait_recv()
        total = jnp.zeros((1, LANES), jnp.float32)
        on_diagonal = (lax.broadcasted_iota(jnp.int32, (LANES, LANES), 0)
                       == lax.broadcasted_iota(jnp.int32, (LANES, LANES), 1))
        for tile in range(width // LANES):
            square = whole[pl.ds(tile * LANES, LANES), pl.ds(tile * LANES, LANES)]
            diagonal = jnp.sum(jnp.where(on_diagonal, square, 0.0), axis=0, keepdims=True)
            total = total + jnp.log(diagonal)
        mean = jnp.sum(total, axis=1, keepdims=True) * (1.0 / width)
        logs[...] = jnp.broadcast_to(mean, logs.shape)
        for step in range(1, n):
            logs_copy(step).start()

        result[...] = rs_ref[...]
        for owner in range(n - 2):
            @pl.when(owner < row - 1)
            def _():
                pltpu.make_async_remote_copy(
                    src_ref=own_part, dst_ref=parts.at[owner], send_sem=part_send, recv_sem=part_recv.at[owner],
                    device_id=(row, solver_col), device_id_type=MESH,
                ).wait_recv()
                result[...] = result[...] - parts[owner]

        @pl.when(row > 0)
        def _():
            y_copy(0).wait_recv()
            result[...] = result[...] - project(arrived[...])

        reduced = result[...].astype(jnp.bfloat16).astype(jnp.float32)
        for right in range(width // 256):
            value = jnp.zeros((reduced.shape[0], 256), jnp.float32)
            for left in range(right + 1):
                value = value + jnp.dot(
                    reduced[:, left * 256:(left + 1) * 256],
                    whole[pl.ds(left * 256, 256), pl.ds(right * 256, 256)],
                    preferred_element_type=jnp.float32,
                )
            result[:, pl.ds(right * 256, 256)] = value
        for target in range(1, n):
            @pl.when(target > row)
            def _():
                y_copy(target).start()
        for step in range(1, n):
            final_copy(step).start()
        finish(result[...], mean)
        for target in range(1, n):
            @pl.when(target > row)
            def _():
                y_copy(target).wait_send()
        for step in range(1, n):
            final_copy(step).wait_send()
            logs_copy(step).wait_send()

    @pl.when(jnp.logical_not(is_solver))
    def _():
        @pl.when(below)
        def _():
            y_copy(0).wait_recv()
            own_part[...] = project(arrived[...])
            part_copy().start()
        for owner in range(n):
            @pl.when(col == owner)
            def _():
                block_copy(owner).wait_send()
        @pl.when(below)
        def _():
            part_copy().wait_send()
        logs_copy(1).wait_recv()
        final_copy(1).wait_recv()
        finish(final[...], logs_in[0:1, 0:1])


def local(n, right_side, inverse_t, u_factor, v_factor, ranks):
    nrhs, width = right_side.shape[2:]
    piece = inverse_t.shape[2]
    rank_max = u_factor.shape[4]
    f32 = jnp.float32
    vmem = pl.BlockSpec(memory_space=pltpu.VMEM)
    dma = pltpu.SemaphoreType.DMA
    white, lik = pl.pallas_call(
        functools.partial(kernel, n),
        out_shape=(jax.ShapeDtypeStruct((nrhs, width), f32), jax.ShapeDtypeStruct((nrhs, 1), f32)),
        in_specs=[vmem, vmem, vmem, vmem, pl.BlockSpec(memory_space=pltpu.SMEM)],
        out_specs=(vmem, vmem),
        scratch_shapes=[
            pltpu.VMEM((piece, width), f32),
            pltpu.VMEM((width, width), f32),
            pltpu.VMEM((nrhs, width), f32),
            pltpu.VMEM((nrhs, width), f32),
            pltpu.VMEM((n, nrhs, width), f32),
            pltpu.VMEM((nrhs, width), f32),
            pltpu.VMEM((nrhs, width), f32),
            pltpu.VMEM((8, LANES), f32),
            pltpu.VMEM((8, LANES), f32),
            dma, dma((n,)), dma((n,)), dma, dma, dma((n,)), dma((n,)), dma, dma((n,)), dma,
        ],
        compiler_params=pltpu.CompilerParams(collective_id=0, has_side_effects=True),
    )(
        right_side.reshape(nrhs, width),
        inverse_t.reshape(piece, width),
        u_factor.reshape(rank_max, width),
        v_factor.reshape(rank_max, width),
        ranks.reshape(1, 1),
    )
    return white.reshape(1, 1, nrhs, width), lik.reshape(1, 1, nrhs)


def solution(mesh):
    return jax.shard_map(
        functools.partial(local, mesh.shape["row"]),
        mesh=mesh,
        in_specs=(
            P(None, "row", None, None),
            P(None, "row", "col", None),
            P(None, "row", None, "col", None, None),
            P(None, "row", None, "col", None, None),
            P(None, "row", None, "col"),
        ),
        out_specs=(P(None, "row", None, None), P(None, "row", None)),
        check_vma=False,
    )
```

time: 719 us -> 86.4 us (0.12); the launches traced: 704 us -> 86.2 us
  blocking collectives: 296 us -> 0 us
  waiting for transfers between devices: 171 us -> 0 us
  starting transfers between devices: 164 us -> 0 us
  Pallas kernels: 0 us -> 82.3 us
  local copies, waits for them, and re-layouts: 37.4 us -> 1.99 us
  other arithmetic: 15.5 us -> 0.63 us
  loops' own time: 12.7 us -> 0 us
    all_to_all x16 -> x0, blocking collectives: 280 us -> none  [from_everyone(): lax.all_to_all(jnp.broadcast_to(array[None], (devices, *array.shape)), ax...]
    all_to_all x32 -> x0, waiting for transfers between devices: 171 us -> none  [the longest x16 103 us: summed_on_arrival(): lax.all_to_all(pieces, axis, split_axis=0, concat_axis=0, tiled=True)]
    all_to_all x32 -> x0, starting transfers between devices: 164 us -> none  [the longest x16 99.1 us: from_everyone(): lax.all_to_all(jnp.broadcast_to(array[None], (devices, *array.shape)), ax...]
    pallas_call x0 -> x1, Pallas kernels: none -> 82.3 us  [local(): pl.pallas_call(functools.partial(kernel, n), out_shape=(jax.ShapeDtypeStr...]
    psum x2 -> x0, blocking collectives: 16.1 us -> none  [one_axis_at_a_time(): return functools.reduce(lax.psum, axes, array)]
    another operation x17 -> x0, loops' own time: 12.7 us -> none  [the longest x1 12.3 us: local(): lax.fori_loop(0, slab, right_step, (empty_rows, jnp.zeros((cycles, nrhs,...]
    while x128 -> x0, local copies, waits for them, and re-layouts: 12.7 us -> none
    broadcast_in_dim x32 -> x0, local copies, waits for them, and re-layouts: 12.3 us -> none  [from_everyone(): jnp.broadcast_to(array[None], (devices, *array.shape))]
  transfers between devices with their start and end apart: 32 -> 0, of which waited for: 32 -> 0; matrix products, arithmetic and copies ran while one was open for 0% -> 0% of each run, Pallas kernels for 0% -> 0%
where the time goes in v1:
time: 86.4 us; the launch traced here: 86.2 us
  Pallas kernels  82.3 us (95%)
  local copies, waits for them, and re-layouts  1.99 us (2%)
  between operations  1.29 us (1%)
    pallas_call x1, Pallas kernels, local(): pl.pallas_call(functools.partial(kernel, n), out_shape=(jax.ShapeDtypeStr...  82.3 us
    unnamed x3, local copies, waits for them, and re-layouts  1.99 us

profile of v1, /device:TPU:225, one launch (start us, length us, event | category | flops | bytes accessed | tf_op | source)
XLA Modules:
  0.0 86.2 jit_solution(14522068260179550283)
XLA Ops:
  1.3 82.3 %shard_map.68 = (f32[4,1024]{1,0:T(4,128)}, f32[4,1]{1,0:T(4,128)}) custom-call(f32[4,1024]{1,0:T(4,128)} %bitcast.11, bf16[64,1024]{1,0:T(8,128)(2,1)} %bitcast.10, bf16[128,1024]{1,0:T(8,128)(2,1)} %bitcast.8, bf16[128,1024]{1,0:T(8,128)(2,1)} %bitcast.9, s32[1,1]{1,0:T(1,128)} %bitcast.7.rank_ref), custom_call_target="tpu_custom_call" | custom-call | tf_op jit(solution)/shard_map/pallas_call | solution.py:187
  83.5 0.0 copy-start
  83.5 0.7 copy-done
  84.2 0.6 reduce
  84.8 1.3 %copy.9 = f32[1,1,4,1024]{3,2,1,0:T(4,128)} copy(f32[1,1,4,1024]{3,2,1,0:T(4,128)} %bitcast.12) | data formatting | bytes 32768
Async XLA Ops:
  83.5 0.7 copy-start

commit v2 on v1

v2 whole, which is shorter than its diff:
```python
import functools
import math

import jax
import jax.numpy as jnp
from jax import lax
from jax.experimental import pallas as pl
from jax.experimental.pallas import tpu as pltpu
from jax.sharding import PartitionSpec as P

MESH = pl.DeviceIdType.MESH
LANES = 128
TILE = 256


def solver_of(row, n):
    return jnp.maximum(row - 1, 0)


def kernel(n, rs_ref, inv_ref, u_ref, v_ref, rank_ref, white_ref, lik_ref,
           block, whole, whole16, folded, padded, arrived, own_part, parts, result, final, logs, logs_parts, logs_in,
           block_send, block_recv, y_send, y_recv, part_send, part_recv,
           final_send, final_recv, log_send, log_recv, logs_send, logs_recv):
    row = lax.axis_index("row")
    col = lax.axis_index("col")
    piece, width = inv_ref.shape
    f32, bf16 = jnp.float32, jnp.bfloat16
    solver_col = solver_of(row, n)
    is_solver = col == solver_col
    first_row = row == 0
    below = col < row

    barrier = pltpu.get_barrier_semaphore()
    for step in range(1, n):
        @pl.when(is_solver)
        def _():
            pl.semaphore_signal(barrier, inc=1, device_id=(row, lax.rem(col + step, n)), device_id_type=MESH)
        @pl.when(is_solver & (row + step < n))
        def _():
            pl.semaphore_signal(barrier, inc=1, device_id=(row + step, row), device_id_type=MESH)
    @pl.when(jnp.logical_not(is_solver))
    def _():
        pl.semaphore_signal(barrier, inc=1, device_id=(row, solver_col), device_id_type=MESH)
    @pl.when(below)
    def _():
        pl.semaphore_signal(barrier, inc=1, device_id=(col, solver_of(col, n)), device_id_type=MESH)

    block[...] = inv_ref[...].astype(f32)
    span = max(piece, LANES)
    base = pl.multiple_of(col * piece // span * span, span)
    offset = col * piece - base
    log_base = pl.multiple_of(col * piece // LANES * LANES, LANES)
    total = jnp.zeros((1, LANES), f32)
    for start in range(0, piece, LANES):
        height = min(LANES, piece - start)
        square = block[pl.ds(start, height), pl.ds(log_base + start, LANES)]
        rows_at = lax.broadcasted_iota(jnp.int32, square.shape, 0) + (col * piece - log_base)
        on_diagonal = rows_at == lax.broadcasted_iota(jnp.int32, square.shape, 1)
        total = total + jnp.sum(jnp.log(jnp.where(on_diagonal, square, 1.0)), axis=0, keepdims=True)
    own_log = jnp.sum(total, axis=1, keepdims=True) * (1.0 / width)
    logs[...] = jnp.broadcast_to(own_log, logs.shape)

    @pl.when(first_row)
    def _():
        padded[...] = jnp.zeros(padded.shape, bf16)
        padded[pl.ds(pl.multiple_of(offset, piece), piece), :] = inv_ref[...]
        own_part[...] = jnp.dot(rs_ref[:, pl.ds(base, span)].astype(bf16), padded[...], preferred_element_type=f32)

    @pl.when(is_solver)
    def _():
        for tile in range(width // TILE):
            whole16[pl.ds(tile * TILE + LANES, LANES), pl.ds(tile * TILE, LANES)] = jnp.zeros((LANES, LANES), bf16)

    partners = jnp.where(is_solver, 2 * (n - 1) - row, 1) + jnp.where(below, 1, 0)
    pl.semaphore_wait(barrier, partners)

    def block_first(owner):
        return owner * piece // LANES * LANES

    def block_copy(owner):
        first = block_first(owner)
        return pltpu.make_async_remote_copy(
            src_ref=block.at[:, pl.ds(first, width - first)],
            dst_ref=whole.at[pl.ds(owner * piece, piece), pl.ds(first, width - first)],
            send_sem=block_send,
            recv_sem=block_recv.at[owner],
            device_id=(row, solver_col),
            device_id_type=MESH,
        )

    def low_rank(y):
        inner = lax.dot_general(y.astype(bf16), v_ref[...], (((1,), (1,)), ((), ())), preferred_element_type=f32)
        keep = lax.broadcasted_iota(jnp.int32, inner.shape, 1) < rank_ref[0, 0]
        return jnp.where(keep, inner, 0.0).astype(bf16)

    def y_copy(target):
        return pltpu.make_async_remote_copy(
            src_ref=result, dst_ref=arrived, send_sem=y_send.at[target], recv_sem=y_recv,
            device_id=(target, row), device_id_type=MESH,
        )

    def part_copy(slot):
        return pltpu.make_async_remote_copy(
            src_ref=own_part, dst_ref=parts.at[slot], send_sem=part_send, recv_sem=part_recv.at[slot],
            device_id=(row, solver_col), device_id_type=MESH,
        )

    def log_copy(slot):
        return pltpu.make_async_remote_copy(
            src_ref=logs, dst_ref=logs_parts.at[slot], send_sem=log_send, recv_sem=log_recv.at[slot],
            device_id=(row, solver_col), device_id_type=MESH,
        )

    def final_copy(step):
        return pltpu.make_async_remote_copy(
            src_ref=result, dst_ref=final, send_sem=final_send.at[step], recv_sem=final_recv,
            device_id=(row, lax.rem(col + step, n)), device_id_type=MESH,
        )

    def logs_copy(step):
        return pltpu.make_async_remote_copy(
            src_ref=logs, dst_ref=logs_in, send_sem=logs_send.at[step], recv_sem=logs_recv,
            device_id=(row, lax.rem(col + step, n)), device_id_type=MESH,
        )

    def finish(y, log_mean):
        quadratic = jnp.sum(y * y, axis=1, keepdims=True) * (1.0 / width)
        lik_ref[...] = -0.5 * quadratic + log_mean - 0.5 * math.log(2.0 * math.pi)
        white_ref[...] = y

    def share_logs():
        for owner in range(n):
            @pl.when(col != owner)
            def _():
                log_copy(owner).wait_recv()
                logs[...] = logs[...] + logs_parts[owner]
        for step in range(1, n):
            logs_copy(step).start()

    def upper(left, right):
        return whole16[pl.ds(left * TILE, TILE), pl.ds(right * TILE, TILE)]

    @pl.when(jnp.logical_not(is_solver))
    def _():
        @pl.when(first_row)
        def _():
            part_copy(col).start()
        for owner in range(n):
            @pl.when((col == owner) & jnp.logical_not(first_row))
            def _():
                block_copy(owner).start()
        log_copy(col).start()

    @pl.when(is_solver)
    def _():
        @pl.when(first_row)
        def _():
            y = own_part[...]
            for owner in range(1, n):
                part_copy(owner).wait_recv()
                y = y + parts[owner]
            result[...] = y

        @pl.when(jnp.logical_not(first_row))
        def _():
            for owner in range(n):
                first = block_first(owner)
                rows = pl.ds(owner * piece, piece)
                columns = pl.ds(first, width - first)
                @pl.when(col != owner)
                def _():
                    block_copy(owner).wait_recv()
                    whole16[rows, columns] = whole[rows, columns].astype(bf16)
                @pl.when(col == owner)
                def _():
                    whole16[rows, columns] = inv_ref[:, columns]
            for right in range(width // TILE):
                value = jnp.zeros((folded.shape[0], TILE), f32)
                for left in range(right + 1):
                    value = value + jnp.dot(
                        u_ref[:, pl.ds(left * TILE, TILE)], upper(left, right), preferred_element_type=f32
                    )
                folded[:, pl.ds(right * TILE, TILE)] = value.astype(bf16)
            share_logs()

            result[...] = rs_ref[...]
            for owner in range(n - 2):
                @pl.when(owner < row - 1)
                def _():
                    part_copy(owner).wait_recv()
                    result[...] = result[...] - parts[owner]
            reduced = result[...].astype(bf16)
            for right in range(width // TILE):
                value = jnp.zeros((reduced.shape[0], TILE), f32)
                for left in range(right + 1):
                    value = value + jnp.dot(
                        reduced[:, left * TILE:(left + 1) * TILE], upper(left, right), preferred_element_type=f32
                    )
                final[:, pl.ds(right * TILE, TILE)] = value

            y_copy(0).wait_recv()
            result[...] = final[...] - jnp.dot(low_rank(arrived[...]), folded[...], preferred_element_type=f32)

        for target in range(1, n):
            @pl.when(target > row)
            def _():
                y_copy(target).start()
        for step in range(1, n):
            final_copy(step).start()
        @pl.when(first_row)
        def _():
            share_logs()
        finish(result[...], logs[0:1, 0:1])
        for target in range(1, n):
            @pl.when(target > row)
            def _():
                y_copy(target).wait_send()
        for step in range(1, n):
            final_copy(step).wait_send()
            logs_copy(step).wait_send()

    @pl.when(jnp.logical_not(is_solver))
    def _():
        @pl.when(below)
        def _():
            y_copy(0).wait_recv()
            own_part[...] = jnp.dot(low_rank(arrived[...]), u_ref[...], preferred_element_type=f32)
            part_copy(col).start()
        for owner in range(n):
            @pl.when((col == owner) & jnp.logical_not(first_row))
            def _():
                block_copy(owner).wait_send()
        log_copy(col).wait_send()
        @pl.when(below | first_row)
        def _():
            part_copy(col).wait_send()
        logs_copy(1).wait_recv()
        final_copy(1).wait_recv()
        finish(final[...], logs_in[0:1, 0:1])


def local(n, right_side, inverse_t, u_factor, v_factor, ranks):
    nrhs, width = right_side.shape[2:]
    piece = inverse_t.shape[2]
    rank_max = u_factor.shape[4]
    f32, bf16 = jnp.float32, jnp.bfloat16
    vmem = pl.BlockSpec(memory_space=pltpu.VMEM)
    dma = pltpu.SemaphoreType.DMA
    rows = pltpu.VMEM((nrhs, width), f32)
    small = pltpu.VMEM((8, LANES), f32)
    white, lik = pl.pallas_call(
        functools.partial(kernel, n),
        out_shape=(jax.ShapeDtypeStruct((nrhs, width), f32), jax.ShapeDtypeStruct((nrhs, 1), f32)),
        in_specs=[vmem, vmem, vmem, vmem, pl.BlockSpec(memory_space=pltpu.SMEM)],
        out_specs=(vmem, vmem),
        scratch_shapes=[
            pltpu.VMEM((piece, width), f32),
            pltpu.VMEM((width, width), f32),
            pltpu.VMEM((width, width), bf16),
            pltpu.VMEM((rank_max, width), bf16),
            pltpu.VMEM((max(piece, LANES), width), bf16),
            rows,
            rows,
            pltpu.VMEM((n, nrhs, width), f32),
            rows,
            rows,
            small,
            pltpu.VMEM((n, 8, LANES), f32),
            small,
            dma, dma((n,)), dma((n,)), dma, dma, dma((n,)), dma((n,)), dma, dma, dma((n,)), dma((n,)), dma,
        ],
        compiler_params=pltpu.CompilerParams(collective_id=0, has_side_effects=True),
    )(
        right_side.reshape(nrhs, width),
        inverse_t.reshape(piece, width),
        u_factor.reshape(rank_max, width),
        v_factor.reshape(rank_max, width),
        ranks.reshape(1, 1),
    )
    return white.reshape(1, 1, nrhs, width), lik.reshape(1, 1, nrhs)


def solution(mesh):
    return jax.shard_map(
        functools.partial(local, mesh.shape["row"]),
        mesh=mesh,
        in_specs=(
            P(None, "row", None, None),
            P(None, "row", "col", None),
            P(None, "row", None, "col", None, None),
            P(None, "row", None, "col", None, None),
            P(None, "row", None, "col"),
        ),
        out_specs=(P(None, "row", None, None), P(None, "row", None)),
        check_vma=False,
    )
```

time: 86.4 us -> 78 us (0.903)
  Pallas kernels: 82.3 us -> 73.9 us
    pallas_call x1, Pallas kernels: 82.3 us -> 73.9 us  [local(): pl.pallas_call(functools.partial(kernel, n), out_shape=(jax.ShapeDtypeStr...]
where the time goes in v2:
time: 78 us; the launch traced here: 77.8 us
  Pallas kernels  73.9 us (95%)
  local copies, waits for them, and re-layouts  1.99 us (3%)
  between operations  1.29 us (2%)
    pallas_call x1, Pallas kernels, local(): pl.pallas_call(functools.partial(kernel, n), out_shape=(jax.ShapeDtypeStr...  73.9 us
    unnamed x3, local copies, waits for them, and re-layouts  1.99 us

profile of v2, /device:TPU:225, one launch (start us, length us, event | category | flops | bytes accessed | tf_op | source)
XLA Modules:
  0.0 77.8 jit_solution(14812032478847944628)
XLA Ops:
  1.3 73.9 %shard_map.68 = (f32[4,1024]{1,0:T(4,128)}, f32[4,1]{1,0:T(4,128)}) custom-call(f32[4,1024]{1,0:T(4,128)} %bitcast.11, bf16[64,1024]{1,0:T(8,128)(2,1)} %bitcast.10, bf16[128,1024]{1,0:T(8,128)(2,1)} %bitcast.8, bf16[128,1024]{1,0:T(8,128)(2,1)} %bitcast.9, s32[1,1]{1,0:T(1,128)} %bitcast.7.rank_ref), custom_call_target="tpu_custom_call" | custom-call | tf_op jit(solution)/shard_map/pallas_call | solution.py:251
  75.2 0.0 copy-start
  75.2 0.7 copy-done
  75.8 0.6 reduce
  76.5 1.3 %copy.9 = f32[1,1,4,1024]{3,2,1,0:T(4,128)} copy(f32[1,1,4,1024]{3,2,1,0:T(4,128)} %bitcast.12) | data formatting | bytes 32768
Async XLA Ops:
  75.2 0.7 copy-start

commit v3 on v2

v3 whole, which is shorter than its diff:
```python
import functools
import math

import jax
import jax.numpy as jnp
from jax import lax
from jax.experimental import pallas as pl
from jax.experimental.pallas import tpu as pltpu
from jax.sharding import PartitionSpec as P

MESH = pl.DeviceIdType.MESH
LANES = 128
TILE = 256
SECOND = 3


def solver_of(row):
    even = lax.rem(row, 2) == 0
    return jnp.where(even & (row > 0), row + 1, row), jnp.maximum(row - 1, 0)


def kernel(n, rs_ref, inv_ref, u_ref, v_ref, rank_ref, white_ref, lik_ref,
           block, whole, whole16, u32, v32, u16, u_near, v_near, v_pair, u_second, rs_near, folded, padded,
           arrived, own_part, parts, own_inner, inner_second, solved, result, final,
           logs, logs_parts, logs_all, logs_in,
           block_send, block_recv, tile_send, tile_recv, inner_send, inner_recv, y_send, y_recv, part_send, part_recv,
           final_send, final_recv, log_send, log_recv, logs_send, logs_recv):
    row = lax.axis_index("row")
    col = lax.axis_index("col")
    piece, width = inv_ref.shape
    rank_max = u_ref.shape[0]
    f32, bf16 = jnp.float32, jnp.bfloat16

    odd = lax.rem(row, 2) == 1
    for_odd = odd & (col == row - 1)
    for_even = odd & (col == row - 2)
    for_first = (row == 0) & (col == 0)
    is_solver = for_odd | for_even | for_first
    mine = jnp.where(for_even, row - 1, row)
    solver = solver_of(row)
    in_row = for_odd | for_first
    first_row = row == 0
    near = col == row - 1
    moved = near & jnp.logical_not(odd)
    second = (col == row - 2) & (row >= SECOND)
    takes_y = (col < row) & jnp.logical_not(moved)
    sends_part = (col < row - 2) | ((col == row - 2) & (row < SECOND))
    is_worker = takes_y & jnp.logical_not(is_solver)

    def feeds(source, target):
        return (target > source) & (target < n) & jnp.logical_not((target == source + 1) & (lax.rem(target, 2) == 0))

    barrier = pltpu.get_barrier_semaphore()
    fed = 0
    for step in range(n):
        in_my_row = is_solver & jnp.logical_not(in_row & (col == step))
        @pl.when(in_my_row)
        def _():
            pl.semaphore_signal(barrier, inc=1, device_id=(mine, step), device_id_type=MESH)
        feeding = is_solver & feeds(mine, step)
        @pl.when(feeding)
        def _():
            pl.semaphore_signal(barrier, inc=1, device_id=(step, mine), device_id_type=MESH)
        fed = fed + in_my_row.astype(jnp.int32) + feeding.astype(jnp.int32)
    @pl.when(jnp.logical_not(in_row))
    def _():
        pl.semaphore_signal(barrier, inc=1, device_id=solver, device_id_type=MESH)
    @pl.when(takes_y)
    def _():
        pl.semaphore_signal(barrier, inc=1, device_id=solver_of(col), device_id_type=MESH)

    block[...] = inv_ref[...].astype(f32)
    keep = lax.broadcasted_iota(jnp.int32, u_ref.shape, 0) < rank_ref[0, 0]
    u32[...] = jnp.where(keep, u_ref[...].astype(f32), 0.0)
    u16[...] = u32[...].astype(bf16)
    @pl.when(moved)
    def _():
        v32[...] = v_ref[...].astype(f32)

    span = max(piece, LANES)
    base = pl.multiple_of(col * piece // span * span, span)
    offset = col * piece - base
    @pl.when(first_row)
    def _():
        padded[...] = jnp.zeros(padded.shape, bf16)
        padded[pl.ds(pl.multiple_of(offset, piece), piece), :] = inv_ref[...]
        own_part[...] = jnp.dot(rs_ref[:, pl.ds(base, span)].astype(bf16), padded[...], preferred_element_type=f32)

    log_base = pl.multiple_of(col * piece // LANES * LANES, LANES)
    total = jnp.zeros((1, LANES), f32)
    for start in range(0, piece, LANES):
        height = min(LANES, piece - start)
        square = block[pl.ds(start, height), pl.ds(log_base + start, LANES)]
        rows_at = lax.broadcasted_iota(jnp.int32, square.shape, 0) + (col * piece - log_base)
        on_diagonal = rows_at == lax.broadcasted_iota(jnp.int32, square.shape, 1)
        total = total + jnp.sum(jnp.log(jnp.where(on_diagonal, square, 1.0)), axis=0, keepdims=True)
    own_log = jnp.sum(total, axis=1, keepdims=True) * (1.0 / width)
    logs[...] = jnp.broadcast_to(own_log, logs.shape)

    @pl.when(is_solver)
    def _():
        for tile in range(width // TILE):
            whole16[pl.ds(tile * TILE + LANES, LANES), pl.ds(tile * TILE, LANES)] = jnp.zeros((LANES, LANES), bf16)

    waits = fed + jnp.where(in_row, 0, 1) + jnp.where(takes_y, 1, 0)
    pl.semaphore_wait(barrier, waits)

    def block_first(owner):
        return owner * piece // LANES * LANES

    def remote(source, target, send, recv, device):
        return pltpu.make_async_remote_copy(
            src_ref=source, dst_ref=target, send_sem=send, recv_sem=recv, device_id=device, device_id_type=MESH
        )

    def block_copy(owner):
        first = block_first(owner)
        return remote(
            block.at[:, pl.ds(first, width - first)],
            whole.at[pl.ds(owner * piece, piece), pl.ds(first, width - first)],
            block_send, block_recv.at[owner], solver,
        )

    def u_copy():
        return remote(u32, u_near, tile_send.at[0], tile_recv.at[0], solver)

    def v_copy():
        return remote(v32, v_near, tile_send.at[1], tile_recv.at[1], solver)

    def rs_copy():
        return remote(rs_ref, rs_near, tile_send.at[2], tile_recv.at[2], solver)

    def second_copy():
        return remote(u32, u_second, tile_send.at[3], tile_recv.at[3], solver)

    def inner_copy():
        return remote(own_inner, inner_second, inner_send, inner_recv, solver)

    def y_copy(target):
        return remote(result, arrived, y_send.at[target], y_recv, (target, mine))

    def part_copy(slot):
        return remote(own_part, parts.at[slot], part_send, part_recv.at[slot], solver)

    def log_copy(slot):
        return remote(logs, logs_parts.at[slot], log_send, log_recv.at[slot], solver)

    def final_copy(target):
        return remote(result, final, final_send.at[target], final_recv, (mine, target))

    def logs_copy(target):
        return remote(logs_all, logs_in, logs_send.at[target], logs_recv, (mine, target))

    def inner_of(y, v):
        return lax.dot_general(y.astype(bf16), v, (((1,), (1,)), ((), ())), preferred_element_type=f32)

    def finish(y, log_mean):
        quadratic = jnp.sum(y * y, axis=1, keepdims=True) * (1.0 / width)
        lik_ref[...] = -0.5 * quadratic + log_mean - 0.5 * math.log(2.0 * math.pi)
        white_ref[...] = y

    def others():
        for target in range(n):
            yield target, jnp.logical_not(in_row & (col == target))

    def share_logs():
        logs_all[...] = jnp.where(in_row, logs[...], 0.0)
        for owner, other in others():
            @pl.when(other)
            def _():
                log_copy(owner).wait_recv()
                logs_all[...] = logs_all[...] + logs_parts[owner]
        for target, other in others():
            @pl.when(other)
            def _():
                logs_copy(target).start()

    def upper(left, right):
        return whole16[pl.ds(left * TILE, TILE), pl.ds(right * TILE, TILE)]

    def times_upper(lhs, right):
        value = jnp.zeros((lhs.shape[0], TILE), f32)
        for left in range(right + 1):
            value = value + jnp.dot(
                lhs[:, left * TILE:(left + 1) * TILE], upper(left, right), preferred_element_type=f32
            )
        return value

    @pl.when(first_row & jnp.logical_not(in_row))
    def _():
        part_copy(col).start()
    for owner in range(n):
        @pl.when((col == owner) & jnp.logical_not(first_row | in_row))
        def _():
            block_copy(owner).start()
    @pl.when(moved)
    def _():
        rs_copy().start()
        v_copy().start()
        u_copy().start()
    @pl.when(second)
    def _():
        second_copy().start()
    @pl.when(jnp.logical_not(in_row))
    def _():
        log_copy(col).start()

    @pl.when(is_solver)
    def _():
        @pl.when(for_first)
        def _():
            y = own_part[...]
            for owner in range(1, n):
                part_copy(owner).wait_recv()
                y = y + parts[owner]
            result[...] = y

        @pl.when(jnp.logical_not(for_first))
        def _():
            @pl.when(for_even)
            def _():
                rs_copy().wait_recv()
                v_copy().wait_recv()
                u_copy().wait_recv()
                u16[...] = u_near[...].astype(bf16)
                v_pair[pl.ds(0, rank_max), :] = v_near[...].astype(bf16)
                v_pair[pl.ds(rank_max, rank_max), :] = v_ref[...]
            @pl.when(for_odd)
            def _():
                rs_near[...] = rs_ref[...]
                v_pair[pl.ds(0, rank_max), :] = v_ref[...]
                v_pair[pl.ds(rank_max, rank_max), :] = v_ref[...]
            for owner in range(n):
                first = block_first(owner)
                rows = pl.ds(owner * piece, piece)
                columns = pl.ds(first, width - first)
                @pl.when(jnp.logical_not(in_row & (col == owner)))
                def _():
                    block_copy(owner).wait_recv()
                    whole16[rows, columns] = whole[rows, columns].astype(bf16)
                @pl.when(in_row & (col == owner))
                def _():
                    whole16[rows, columns] = inv_ref[:, columns]
            for right in range(width // TILE):
                folded[pl.ds(0, rank_max), pl.ds(right * TILE, TILE)] = times_upper(u16, right).astype(bf16)
            @pl.when(mine >= SECOND)
            def _():
                second_copy().wait_recv()
                u16[...] = u_second[...].astype(bf16)
                for right in range(width // TILE):
                    folded[pl.ds(rank_max, rank_max), pl.ds(right * TILE, TILE)] = times_upper(u16, right).astype(bf16)
            @pl.when(mine < SECOND)
            def _():
                folded[pl.ds(rank_max, rank_max), :] = jnp.zeros((rank_max, width), bf16)
            share_logs()

            result[...] = rs_near[...]
            for owner in range(n - 2):
                @pl.when((owner < mine - 2) | ((owner < mine - 1) & (mine < SECOND)))
                def _():
                    part_copy(owner).wait_recv()
                    result[...] = result[...] - parts[owner]
            reduced = result[...].astype(bf16)
            for right in range(width // TILE):
                solved[:, pl.ds(right * TILE, TILE)] = times_upper(reduced, right)

            y_copy(0).wait_recv()
            inner = inner_of(arrived[...], v_pair[...])
            @pl.when(for_even & second)
            def _():
                own_inner[...] = inner[:, rank_max:]
                inner_copy().start()
            @pl.when(for_even & sends_part)
            def _():
                own_part[...] = jnp.dot(inner[:, rank_max:].astype(bf16), u32[...].astype(bf16), preferred_element_type=f32)
                part_copy(col).start()
            @pl.when(mine >= SECOND)
            def _():
                inner_copy().wait_recv()
            @pl.when(mine < SECOND)
            def _():
                inner_second[...] = jnp.zeros(inner_second.shape, f32)
            result[...] = solved[...] - jnp.dot(
                jnp.concatenate([inner[:, :rank_max], inner_second[...]], axis=1).astype(bf16),
                folded[...], preferred_element_type=f32,
            )

        for target in range(1, n):
            @pl.when(feeds(mine, target))
            def _():
                y_copy(target).start()
        for target, other in others():
            @pl.when(other)
            def _():
                final_copy(target).start()
        @pl.when(for_first)
        def _():
            share_logs()

    @pl.when(is_worker)
    def _():
        y_copy(0).wait_recv()
        inner = inner_of(arrived[...], v_ref[...])
        @pl.when(second)
        def _():
            own_inner[...] = inner
            inner_copy().start()
        @pl.when(sends_part)
        def _():
            own_part[...] = jnp.dot(inner.astype(bf16), u16[...], preferred_element_type=f32)
            part_copy(col).start()

    @pl.when(in_row)
    def _():
        finish(result[...], logs_all[0:1, 0:1])
    @pl.when(jnp.logical_not(in_row))
    def _():
        logs_copy(0).wait_recv()
        final_copy(0).wait_recv()
        finish(final[...], logs_in[0:1, 0:1])

    for owner in range(n):
        @pl.when((col == owner) & jnp.logical_not(first_row | in_row))
        def _():
            block_copy(owner).wait_send()
    @pl.when(moved)
    def _():
        rs_copy().wait_send()
        v_copy().wait_send()
        u_copy().wait_send()
    @pl.when(second)
    def _():
        second_copy().wait_send()
        inner_copy().wait_send()
    @pl.when(jnp.logical_not(in_row))
    def _():
        log_copy(col).wait_send()
    @pl.when(sends_part | (first_row & jnp.logical_not(in_row)))
    def _():
        part_copy(col).wait_send()
    @pl.when(is_solver)
    def _():
        for target in range(1, n):
            @pl.when(feeds(mine, target))
            def _():
                y_copy(target).wait_send()
        for target, other in others():
            @pl.when(other)
            def _():
                final_copy(target).wait_send()
                logs_copy(target).wait_send()


def local(n, right_side, inverse_t, u_factor, v_factor, ranks):
    nrhs, width = right_side.shape[2:]
    piece = inverse_t.shape[2]
    rank_max = u_factor.shape[4]
    f32, bf16 = jnp.float32, jnp.bfloat16
    vmem = pl.BlockSpec(memory_space=pltpu.VMEM)
    dma = pltpu.SemaphoreType.DMA
    rows = pltpu.VMEM((nrhs, width), f32)
    small = pltpu.VMEM((8, LANES), f32)
    factor32 = pltpu.VMEM((rank_max, width), f32)
    factor16 = pltpu.VMEM((rank_max, width), bf16)
    inner = pltpu.VMEM((nrhs, rank_max), f32)
    white, lik = pl.pallas_call(
        functools.partial(kernel, n),
        out_shape=(jax.ShapeDtypeStruct((nrhs, width), f32), jax.ShapeDtypeStruct((nrhs, 1), f32)),
        in_specs=[vmem, vmem, vmem, vmem, pl.BlockSpec(memory_space=pltpu.SMEM)],
        out_specs=(vmem, vmem),
        scratch_shapes=[
            pltpu.VMEM((piece, width), f32),
            pltpu.VMEM((width, width), f32),
            pltpu.VMEM((width, width), bf16),
            factor32,
            factor32,
            factor16,
            factor32,
            factor32,
            pltpu.VMEM((2 * rank_max, width), bf16),
            factor32,
            rows,
            pltpu.VMEM((2 * rank_max, width), bf16),
            pltpu.VMEM((max(piece, LANES), width), bf16),
            rows,
            rows,
            pltpu.VMEM((n, nrhs, width), f32),
            inner,
            inner,
            rows,
            rows,
            rows,
            small,
            pltpu.VMEM((n, 8, LANES), f32),
            small,
            small,
            dma, dma((n,)), dma((4,)), dma((4,)), dma, dma, dma((n,)), dma, dma, dma((n,)),
            dma((n,)), dma, dma, dma((n,)), dma((n,)), dma,
        ],
        compiler_params=pltpu.CompilerParams(collective_id=0, has_side_effects=True),
    )(
        right_side.reshape(nrhs, width),
        inverse_t.reshape(piece, width),
        u_factor.reshape(rank_max, width),
        v_factor.reshape(rank_max, width),
        ranks.reshape(1, 1),
    )
    return white.reshape(1, 1, nrhs, width), lik.reshape(1, 1, nrhs)


def solution(mesh):
    return jax.shard_map(
        functools.partial(local, mesh.shape["row"]),
        mesh=mesh,
        in_specs=(
            P(None, "row", None, None),
            P(None, "row", "col", None),
            P(None, "row", None, "col", None, None),
            P(None, "row", None, "col", None, None),
            P(None, "row", None, "col"),
        ),
        out_specs=(P(None, "row", None, None), P(None, "row", None)),
        check_vma=False,
    )
```

time: 78 us -> 69.8 us (0.89)
  Pallas kernels: 73.9 us -> 65.7 us
    pallas_call x1, Pallas kernels: 73.9 us -> 65.7 us  [local(): pl.pallas_call(functools.partial(kernel, n), out_shape=(jax.ShapeDtypeStr...]
where the time goes in v3:
time: 69.8 us; the launch traced here: 69.6 us
  Pallas kernels  65.7 us (94%)
  local copies, waits for them, and re-layouts  1.99 us (3%)
  between operations  1.29 us (2%)
    pallas_call x1, Pallas kernels, local(): pl.pallas_call(functools.partial(kernel, n), out_shape=(jax.ShapeDtypeStr...  65.7 us
    unnamed x3, local copies, waits for them, and re-layouts  1.99 us

profile of v3, /device:TPU:225, one launch (start us, length us, event | category | flops | bytes accessed | tf_op | source)
XLA Modules:
  0.0 69.6 jit_solution(6354930493336856290)
XLA Ops:
  1.3 65.7 %shard_map.68 = (f32[4,1024]{1,0:T(4,128)}, f32[4,1]{1,0:T(4,128)}) custom-call(f32[4,1024]{1,0:T(4,128)} %bitcast.11, bf16[64,1024]{1,0:T(8,128)(2,1)} %bitcast.10, bf16[128,1024]{1,0:T(8,128)(2,1)} %bitcast.8, bf16[128,1024]{1,0:T(8,128)(2,1)} %bitcast.9, s32[1,1]{1,0:T(1,128)} %bitcast.7.rank_ref), custom_call_target="tpu_custom_call" | custom-call | tf_op jit(solution)/shard_map/pallas_call | solution.py:366
  67.0 0.0 copy-start
  67.0 0.7 copy-done
  67.7 0.6 reduce
  68.3 1.3 %copy.9 = f32[1,1,4,1024]{3,2,1,0:T(4,128)} copy(f32[1,1,4,1024]{3,2,1,0:T(4,128)} %bitcast.12) | data formatting | bytes 32768
Async XLA Ops:
  67.0 0.7 copy-start

commit v4 on v3

--- a/solution.py
+++ b/solution.py
@@ -11,7 +11,7 @@
 MESH = pl.DeviceIdType.MESH
 LANES = 128
 TILE = 256
-SECOND = 3
+SECOND = 4
 
 
 def solver_of(row):
@@ -21,7 +21,7 @@
 
 def kernel(n, rs_ref, inv_ref, u_ref, v_ref, rank_ref, white_ref, lik_ref,
            block, whole, whole16, u32, v32, u16, u_near, v_near, v_pair, u_second, rs_near, folded, padded,
-           arrived, own_part, parts, own_inner, inner_second, solved, result, final,
+           lhs, products, arrived, own_part, parts, own_inner, inner_second, solved, result, final,
            logs, logs_parts, logs_all, logs_in,
            block_send, block_recv, tile_send, tile_recv, inner_send, inner_recv, y_send, y_recv, part_send, part_recv,
            final_send, final_recv, log_send, log_recv, logs_send, logs_recv):
@@ -29,6 +29,7 @@
     col = lax.axis_index("col")
     piece, width = inv_ref.shape
     rank_max = u_ref.shape[0]
+    nrhs = rs_ref.shape[0]
     f32, bf16 = jnp.float32, jnp.bfloat16
 
     odd = lax.rem(row, 2) == 1
@@ -136,8 +137,8 @@
     def inner_copy():
         return remote(own_inner, inner_second, inner_send, inner_recv, solver)
 
-    def y_copy(target):
-        return remote(result, arrived, y_send.at[target], y_recv, (target, mine))
+    def y_copy(step):
+        return remote(result, arrived, y_send.at[step], y_recv, (mine + step, mine))
 
     def part_copy(slot):
         return remote(own_part, parts.at[slot], part_send, part_recv.at[slot], solver)
@@ -155,9 +156,11 @@
         return lax.dot_general(y.astype(bf16), v, (((1,), (1,)), ((), ())), preferred_element_type=f32)
 
     def finish(y, log_mean):
-        quadratic = jnp.sum(y * y, axis=1, keepdims=True) * (1.0 / width)
-        lik_ref[...] = -0.5 * quadratic + log_mean - 0.5 * math.log(2.0 * math.pi)
+        lik_ref[...] = log_mean
         white_ref[...] = y
+
+    def update(inner, depth):
+        result[...] = solved[...] - jnp.dot(inner, folded[pl.ds(0, depth), :], preferred_element_type=f32)
 
     def others():
         for target in range(n):
@@ -223,77 +226,96 @@
                 v_copy().wait_recv()
                 u_copy().wait_recv()
                 u16[...] = u_near[...].astype(bf16)
-                v_pair[pl.ds(0, rank_max), :] = v_near[...].astype(bf16)
-                v_pair[pl.ds(rank_max, rank_max), :] = v_ref[...]
+                v_pair[:, pl.ds(0, rank_max)] = v_near[...].T.astype(bf16)
+                v_pair[:, pl.ds(rank_max, rank_max)] = v_ref[...].astype(f32).T.astype(bf16)
             @pl.when(for_odd)
             def _():
                 rs_near[...] = rs_ref[...]
-                v_pair[pl.ds(0, rank_max), :] = v_ref[...]
-                v_pair[pl.ds(rank_max, rank_max), :] = v_ref[...]
-            for owner in range(n):
-                first = block_first(owner)
-                rows = pl.ds(owner * piece, piece)
-                columns = pl.ds(first, width - first)
-                @pl.when(jnp.logical_not(in_row & (col == owner)))
-                def _():
-                    block_copy(owner).wait_recv()
-                    whole16[rows, columns] = whole[rows, columns].astype(bf16)
-                @pl.when(in_row & (col == owner))
-                def _():
-                    whole16[rows, columns] = inv_ref[:, columns]
-            for right in range(width // TILE):
-                folded[pl.ds(0, rank_max), pl.ds(right * TILE, TILE)] = times_upper(u16, right).astype(bf16)
+                v_pair[:, pl.ds(0, rank_max)] = v_ref[...].astype(f32).T.astype(bf16)
+            lhs[pl.ds(0, rank_max), :] = u16[...]
+            lhs[pl.ds(rank_max, 16), :] = jnp.concatenate([rs_near[...]] * (16 // nrhs), axis=0).astype(bf16)
+            for left in range(width // TILE):
+                for owner in range(left * TILE // piece, (left + 1) * TILE // piece):
+                    first = block_first(owner)
+                    rows = pl.ds(owner * piece, piece)
+                    columns = pl.ds(first, width - first)
+                    @pl.when(jnp.logical_not(in_row & (col == owner)))
+                    def _():
+                        block_copy(owner).wait_recv()
+                        whole16[rows, columns] = whole[rows, columns].astype(bf16)
+                    @pl.when(in_row & (col == owner))
+                    def _():
+                        whole16[rows, columns] = inv_ref[:, columns]
+                for right in range(left, width // TILE):
+                    value = jnp.dot(lhs[:, pl.ds(left * TILE, TILE)], upper(left, right), preferred_element_type=f32)
+                    columns = pl.ds(right * TILE, TILE)
+                    if left:
+                        value = value + products[:, columns]
+                    products[:, columns] = value
+            folded[pl.ds(0, rank_max), :] = products[pl.ds(0, rank_max), :].astype(bf16)
             @pl.when(mine >= SECOND)
             def _():
                 second_copy().wait_recv()
                 u16[...] = u_second[...].astype(bf16)
                 for right in range(width // TILE):
                     folded[pl.ds(rank_max, rank_max), pl.ds(right * TILE, TILE)] = times_upper(u16, right).astype(bf16)
-            @pl.when(mine < SECOND)
-            def _():
-                folded[pl.ds(rank_max, rank_max), :] = jnp.zeros((rank_max, width), bf16)
-            share_logs()
-
-            result[...] = rs_near[...]
-            for owner in range(n - 2):
-                @pl.when((owner < mine - 2) | ((owner < mine - 1) & (mine < SECOND)))
-                def _():
-                    part_copy(owner).wait_recv()
-                    result[...] = result[...] - parts[owner]
-            reduced = result[...].astype(bf16)
-            for right in range(width // TILE):
-                solved[:, pl.ds(right * TILE, TILE)] = times_upper(reduced, right)
-
-            y_copy(0).wait_recv()
-            inner = inner_of(arrived[...], v_pair[...])
-            @pl.when(for_even & second)
-            def _():
+
+            @pl.when(mine == 1)
+            def _():
+                solved[...] = products[pl.ds(rank_max, nrhs), :]
+            @pl.when(mine > 1)
+            def _():
+                share_logs()
+                result[...] = rs_near[...]
+                for owner in range(n - 2):
+                    @pl.when((owner < mine - 2) | ((owner < mine - 1) & (mine < SECOND)))
+                    def _():
+                        part_copy(owner).wait_recv()
+                        result[...] = result[...] - parts[owner]
+                reduced = result[...].astype(bf16)
+                for right in range(width // TILE):
+                    solved[:, pl.ds(right * TILE, TILE)] = times_upper(reduced, right)
+
+            two = mine >= SECOND
+            @pl.when(for_odd & jnp.logical_not(two))
+            def _():
+                y_copy(0).wait_recv()
+                inner = jnp.dot(arrived[...].astype(bf16), v_pair[:, pl.ds(0, rank_max)], preferred_element_type=f32)
+                update(inner.astype(bf16), rank_max)
+            @pl.when(for_even & jnp.logical_not(two))
+            def _():
+                y_copy(0).wait_recv()
+                inner = jnp.dot(arrived[...].astype(bf16), v_pair[...], preferred_element_type=f32)
+                own_inner[...] = inner[:, rank_max:]
+                update(inner[:, :rank_max].astype(bf16), rank_max)
+            @pl.when(for_odd & two)
+            def _():
+                y_copy(0).wait_recv()
+                inner_copy().wait_recv()
+                inner = jnp.dot(arrived[...].astype(bf16), v_pair[:, pl.ds(0, rank_max)], preferred_element_type=f32)
+                update(jnp.concatenate([inner, inner_second[...]], axis=1).astype(bf16), 2 * rank_max)
+            @pl.when(for_even & two)
+            def _():
+                y_copy(0).wait_recv()
+                inner = jnp.dot(arrived[...].astype(bf16), v_pair[...], preferred_element_type=f32)
                 own_inner[...] = inner[:, rank_max:]
                 inner_copy().start()
-            @pl.when(for_even & sends_part)
-            def _():
-                own_part[...] = jnp.dot(inner[:, rank_max:].astype(bf16), u32[...].astype(bf16), preferred_element_type=f32)
-                part_copy(col).start()
-            @pl.when(mine >= SECOND)
-            def _():
                 inner_copy().wait_recv()
-            @pl.when(mine < SECOND)
-            def _():
-                inner_second[...] = jnp.zeros(inner_second.shape, f32)
-            result[...] = solved[...] - jnp.dot(
-                jnp.concatenate([inner[:, :rank_max], inner_second[...]], axis=1).astype(bf16),
-                folded[...], preferred_element_type=f32,
-            )
-
-        for target in range(1, n):
-            @pl.when(feeds(mine, target))
-            def _():
-                y_copy(target).start()
+                update(jnp.concatenate([inner[:, :rank_max], inner_second[...]], axis=1).astype(bf16), 2 * rank_max)
+
+        for step in range(1, n):
+            @pl.when(feeds(mine, mine + step))
+            def _():
+                y_copy(step).start()
         for target, other in others():
             @pl.when(other)
             def _():
                 final_copy(target).start()
-        @pl.when(for_first)
+        @pl.when(for_even & sends_part)
+        def _():
+            own_part[...] = jnp.dot(own_inner[...].astype(bf16), u32[...].astype(bf16), preferred_element_type=f32)
+            part_copy(col).start()
+        @pl.when(mine <= 1)
         def _():
             share_logs()
 
@@ -312,12 +334,12 @@
 
     @pl.when(in_row)
     def _():
-        finish(result[...], logs_all[0:1, 0:1])
+        finish(result[...], logs_all[...])
     @pl.when(jnp.logical_not(in_row))
     def _():
         logs_copy(0).wait_recv()
         final_copy(0).wait_recv()
-        finish(final[...], logs_in[0:1, 0:1])
+        finish(final[...], logs_in[...])
 
     for owner in range(n):
         @pl.when((col == owner) & jnp.logical_not(first_row | in_row))
@@ -340,15 +362,24 @@
         part_copy(col).wait_send()
     @pl.when(is_solver)
     def _():
-        for target in range(1, n):
-            @pl.when(feeds(mine, target))
-            def _():
-                y_copy(target).wait_send()
+        for step in range(1, n):
+            @pl.when(feeds(mine, mine + step))
+            def _():
+                y_copy(step).wait_send()
         for target, other in others():
             @pl.when(other)
             def _():
                 final_copy(target).wait_send()
                 logs_copy(target).wait_send()
+
+
+def outputs(y_ref, log_ref, white_ref, lik_ref):
+    y = y_ref[...]
+    nrhs, width = y.shape
+    lik = -0.5 * jnp.sum(y * y, axis=1, keepdims=True) * (1.0 / width) + log_ref[0:1, 0:1] - 0.5 * math.log(2.0 * math.pi)
+    diagonal = lax.broadcasted_iota(jnp.int32, (nrhs, nrhs), 0) == lax.broadcasted_iota(jnp.int32, (nrhs, nrhs), 1)
+    lik_ref[...] = jnp.sum(jnp.where(diagonal, lik, 0.0), axis=0, keepdims=True)
+    white_ref[...] = y
 
 
 def local(n, right_side, inverse_t, u_factor, v_factor, ranks):
@@ -363,9 +394,9 @@
     factor32 = pltpu.VMEM((rank_max, width), f32)
     factor16 = pltpu.VMEM((rank_max, width), bf16)
     inner = pltpu.VMEM((nrhs, rank_max), f32)
-    white, lik = pl.pallas_call(
+    y, log_mean = pl.pallas_call(
         functools.partial(kernel, n),
-        out_shape=(jax.ShapeDtypeStruct((nrhs, width), f32), jax.ShapeDtypeStruct((nrhs, 1), f32)),
+        out_shape=(jax.ShapeDtypeStruct((nrhs, width), f32), jax.ShapeDtypeStruct((8, LANES), f32)),
         in_specs=[vmem, vmem, vmem, vmem, pl.BlockSpec(memory_space=pltpu.SMEM)],
         out_specs=(vmem, vmem),
         scratch_shapes=[
@@ -377,11 +408,13 @@
             factor16,
             factor32,
             factor32,
-            pltpu.VMEM((2 * rank_max, width), bf16),
+            pltpu.VMEM((width, 2 * rank_max), bf16),
             factor32,
             rows,
             pltpu.VMEM((2 * rank_max, width), bf16),
             pltpu.VMEM((max(piece, LANES), width), bf16),
+            pltpu.VMEM((rank_max + 16, width), bf16),
+            pltpu.VMEM((rank_max + 16, width), f32),
             rows,
             rows,
             pltpu.VMEM((n, nrhs, width), f32),
@@ -405,6 +438,12 @@
         v_factor.reshape(rank_max, width),
         ranks.reshape(1, 1),
     )
+    white, lik = pl.pallas_call(
+        outputs,
+        out_shape=(jax.ShapeDtypeStruct((nrhs, width), f32), jax.ShapeDtypeStruct((1, nrhs), f32)),
+        in_specs=[vmem, vmem],
+        out_specs=(vmem, vmem),
+    )(y, log_mean)
     return white.reshape(1, 1, nrhs, width), lik.reshape(1, 1, nrhs)
 
 

time: 69.8 us -> 65.9 us (0.944)
  local copies, waits for them, and re-layouts: 1.99 us -> 0 us
  Pallas kernels: 65.7 us -> 64.4 us
    pallas_call x1, Pallas kernels: 65.7 us -> 63 us  [local(): pl.pallas_call(functools.partial(kernel, n), out_shape=(jax.ShapeDtypeStr...]
    unnamed x3 -> x0, local copies, waits for them, and re-layouts: 1.99 us -> none
    pallas_call x0 -> x1, Pallas kernels: none -> 1.4 us  [local(): pl.pallas_call(outputs, out_shape=(jax.ShapeDtypeStruct((nrhs, width), f3...]
where the time goes in v4:
time: 65.9 us; the launch traced here: 65.7 us
  Pallas kernels  64.4 us (98%)
  between operations  1.29 us (2%)
    pallas_call x1, Pallas kernels, local(): pl.pallas_call(functools.partial(kernel, n), out_shape=(jax.ShapeDtypeStr...  63 us
    pallas_call x1, Pallas kernels, local(): pl.pallas_call(outputs, out_shape=(jax.ShapeDtypeStruct((nrhs, width), f3...  1.4 us

profile of v4, /device:TPU:225, one launch (start us, length us, event | category | flops | bytes accessed | tf_op | source)
XLA Modules:
  0.0 65.7 jit_solution(1905716926283200771)
XLA Ops:
  1.3 63.0 %shard_map.68 = (f32[4,1024]{1,0:T(4,128)}, f32[8,128]{1,0:T(8,128)}) custom-call(f32[4,1024]{1,0:T(4,128)} %bitcast.11, bf16[64,1024]{1,0:T(8,128)(2,1)} %bitcast.10, bf16[128,1024]{1,0:T(8,128)(2,1)} %bitcast.8, bf16[128,1024]{1,0:T(8,128)(2,1)} %bitcast.9, s32[1,1]{1,0:T(1,128)} %bitcast.7.rank_ref), custom_call_target="tpu_custom_call" | custom-call | tf_op jit(solution)/shard_map/pallas_call | solution.py:397
  64.3 1.4 %shard_map.69 = (f32[4,1024]{1,0:T(4,128)}, f32[1,4]{1,0:T(1,128)}) custom-call(f32[4,1024]{1,0:T(4,128)} %get-tuple-element.6.y_ref, f32[8,128]{1,0:T(8,128)} %get-tuple-element.7.log_ref), custom_call_target="tpu_custom_call" | custom-call | tf_op jit(solution)/shard_map/pallas_call | solution.py:441

commit v5 on v4

v5 whole, which is shorter than its diff:
```python
import functools
import math

import jax
import jax.numpy as jnp
from jax import lax
from jax.experimental import pallas as pl
from jax.experimental.pallas import tpu as pltpu
from jax.sharding import PartitionSpec as P

MESH = pl.DeviceIdType.MESH
LANES = 128
TILE = 256
SECOND = 4


def first_pair(n):
    return 10 if n == 16 else 2


def lean(base, n):
    return 2 - lax.rem(base // 2, 2) if n == 16 else LEAN


LEAN = 1


def solver_of(row, n):
    parity = lax.rem(row, 2)
    base = row - parity
    paired = row >= first_pair(n)
    return (jnp.where((parity == 0) & (row > 0), row + 1, row),
            jnp.where(paired, base - lean(base, n), jnp.maximum(row - 1, 0)))


def kernel(n, rs_ref, inv_ref, u_ref, v_ref, rank_ref, white_ref, lik_ref,
           block, whole, whole16, u32, v32, u16, u_near, v_near, v_pair, v_pair2, v_last, factors, sums, u_second, rs_near,
           tiles, relay, folded, folded2, padded, lhs, products,
           arrived, arrived2, own_part, low_part, parts, own_inner, inner_second, held, solved, result, final,
           logs, logs_parts, logs_all, logs_in,
           block_send, block_recv, tile_send, tile_recv, inner_send, inner_recv, y_send, y_recv, extra_send, extra_recv,
           part_send, part_recv, final_send, final_recv, log_send, log_recv, logs_send, logs_recv,
           relay_send, relay_recv, tiles_send, tiles_recv):
    row = lax.axis_index("row")
    col = lax.axis_index("col")
    piece, width = inv_ref.shape
    rank_max = u_ref.shape[0]
    nrhs = rs_ref.shape[0]
    f32, bf16 = jnp.float32, jnp.bfloat16
    start_pairs = first_pair(n)
    shift = 4 if n == 16 else LEAN + 1

    parity = lax.rem(row, 2)
    odd = parity == 1
    paired = row >= start_pairs
    single = jnp.logical_not(paired)
    pair_row = row - parity
    own_col = pair_row - lean(pair_row, n)
    other_col = pair_row - 3 + lean(pair_row, n)
    pair = odd & (col == own_col) & paired
    for_odd = odd & (col == row - 1) & single
    for_even = odd & (col == row - 2) & single
    for_first = (row == 0) & (col == 0)
    is_single = for_odd | for_even | for_first
    is_solver = is_single | pair
    mine = jnp.where(for_even | pair, row - 1, row)
    kind = lax.rem(mine, 2)
    served = ((0, mine, is_solver), (1, row, pair))
    solver = solver_of(row, n)
    in_row = for_odd | for_first | pair
    first_row = row == 0
    near = col == row - 1
    moved = jnp.where(paired, col == own_col, near) & jnp.logical_not(odd)
    second = (col == row - 2) & (row >= SECOND) & single
    by_x = paired & odd & near
    by_up = paired & jnp.logical_not(odd) & (col == other_col)
    by_down = paired & odd & (col == other_col)
    by_relay = by_x | by_up | by_down
    far = paired & (col <= pair_row - 3)
    lent = far & jnp.logical_not(odd)
    double = far & odd
    takes_y = jnp.where(paired, double | pair, (col < row) & jnp.logical_not(moved))
    sends_part = single & ((col < row - 2) | ((col == row - 2) & (row < SECOND)))
    is_worker = takes_y & single & jnp.logical_not(is_solver)
    relay_row = jnp.where(by_x, row, jnp.where(by_up, lax.rem(row + 2, n), row - 2))
    relay_col = jnp.where(by_x, lax.rem(own_col + shift, n), own_col)
    up_row = lax.rem(row + n - 2, n)
    x_relay = paired & odd & (col == lax.rem(own_col + shift, n))
    up_relay = jnp.logical_not(odd) & (up_row >= start_pairs) & (col == up_row - lean(up_row, n))
    down_relay = odd & (row + 2 > start_pairs) & (row + 2 < n) & (col == row + 1 - lean(row + 1, n))
    is_relay = x_relay | up_relay | down_relay
    from_row = jnp.where(x_relay, row, jnp.where(up_relay, up_row, row + 2))
    from_col = jnp.where(
        x_relay, row - 1, jnp.where(up_relay, up_row - 3 + lean(up_row, n), row - 2 + lean(row + 1, n))
    )
    onto_slot = jnp.where(x_relay, 0, jnp.where(up_relay, 1, 2))

    def feeds(source, target):
        base = target - lax.rem(target, 2)
        early = jnp.logical_not((target == source + 1) & (lax.rem(target, 2) == 0))
        late = ((source <= base - 3) | (source == base - lean(base, n))) & (lax.rem(target, 2) == 1)
        return (target > source) & (target < n) & jnp.where(target >= start_pairs, late, early)

    def next_base(source):
        return source + 2 - lax.rem(source, 2)

    def feeds_extra(source):
        base = next_base(source)
        return (base >= start_pairs) & (base < n) & (source != base - lean(base, n))

    def extra_target(source):
        base = next_base(source)
        return base + 1, base - lean(base, n)

    barrier = pltpu.get_barrier_semaphore()

    def greet(condition, device):
        @pl.when(condition)
        def _():
            pl.semaphore_signal(barrier, inc=1, device_id=device, device_id_type=MESH)
        return condition.astype(jnp.int32)

    waits = 0
    for slot, source, active in served:
        @pl.when(active)
        def _():
            for step in range(n):
                greet(jnp.logical_not((source == row) & (col == step)), (source, step))
            for step in range(1, n):
                greet(feeds(source, source + step), (source + step, source))
            greet(feeds_extra(source), extra_target(source))
        met = n - (source == row).astype(jnp.int32) + feeds_extra(source).astype(jnp.int32)
        for step in range(1, n):
            met = met + feeds(source, source + step).astype(jnp.int32)
        waits = waits + jnp.where(active, met, 0)
    waits = waits + greet(jnp.logical_not(in_row), solver)
    waits = waits + greet(takes_y, solver_of(col, n))
    @pl.when(paired)
    def _():
        greet(pair, solver_of(other_col, n))
        greet(by_relay, (relay_row, relay_col))
        greet(lent, (row + 1, col))
        greet(double, (row - 1, col))
        greet(pair, (row, lax.rem(own_col + shift, n)))
        greet(pair, (lax.rem(row + 1, n), col))
        greet(pair, (row - 2, col))
    @pl.when(is_relay)
    def _():
        greet(is_relay, (from_row, from_col))
        greet(is_relay, solver_of(from_row, n))
    for count, condition in ((4, pair), (1, by_relay), (1, lent), (1, double), (2, is_relay)):
        waits = waits + jnp.where(condition, count, 0)

    block[...] = inv_ref[...].astype(f32)
    keep = lax.broadcasted_iota(jnp.int32, u_ref.shape, 0) < rank_ref[0, 0]
    u32[...] = jnp.where(keep, u_ref[...].astype(f32), 0.0)
    u16[...] = u32[...].astype(bf16)
    @pl.when(moved | by_relay | lent)
    def _():
        v32[...] = v_ref[...].astype(f32)

    span = max(piece, LANES)
    base = pl.multiple_of(col * piece // span * span, span)
    offset = col * piece - base
    @pl.when(first_row)
    def _():
        padded[...] = jnp.zeros(padded.shape, bf16)
        padded[pl.ds(pl.multiple_of(offset, piece), piece), :] = inv_ref[...]
        own_part[...] = jnp.dot(rs_ref[:, pl.ds(base, span)].astype(bf16), padded[...], preferred_element_type=f32)

    log_base = pl.multiple_of(col * piece // LANES * LANES, LANES)
    total = jnp.zeros((1, LANES), f32)
    for start in range(0, piece, LANES):
        height = min(LANES, piece - start)
        square = block[pl.ds(start, height), pl.ds(log_base + start, LANES)]
        rows_at = lax.broadcasted_iota(jnp.int32, square.shape, 0) + (col * piece - log_base)
        on_diagonal = rows_at == lax.broadcasted_iota(jnp.int32, square.shape, 1)
        total = total + jnp.sum(jnp.log(jnp.where(on_diagonal, square, 1.0)), axis=0, keepdims=True)
    own_log = jnp.sum(total, axis=1, keepdims=True) * (1.0 / width)
    logs[...] = jnp.broadcast_to(own_log, logs.shape)

    @pl.when(is_solver)
    def _():
        for half in range(2):
            for tile in range(width // TILE):
                whole16[half, pl.ds(tile * TILE + LANES, LANES), pl.ds(tile * TILE, LANES)] = jnp.zeros(
                    (LANES, LANES), bf16
                )

    pl.semaphore_wait(barrier, waits)

    def block_first(owner):
        return owner * piece // LANES * LANES

    def remote(source, target, send, recv, device):
        return pltpu.make_async_remote_copy(
            src_ref=source, dst_ref=target, send_sem=send, recv_sem=recv, device_id=device, device_id_type=MESH
        )

    def block_copy(owner, half):
        first = block_first(owner)
        return remote(
            block.at[:, pl.ds(first, width - first)],
            whole.at[half, pl.ds(owner * piece, piece), pl.ds(first, width - first)],
            block_send, block_recv.at[half, owner], solver,
        )

    tile_device = (jnp.where(lent, row + 1, solver[0]), jnp.where(lent, col, solver[1]))

    def u_copy():
        return remote(u32, u_near, tile_send.at[0], tile_recv.at[0], tile_device)

    def v_copy():
        return remote(v32, v_near, tile_send.at[1], tile_recv.at[1], tile_device)

    def rs_copy():
        return remote(rs_ref, rs_near, tile_send.at[2], tile_recv.at[2], solver)

    def second_copy():
        return remote(u32, u_second, tile_send.at[3], tile_recv.at[3], solver)

    def relay_copy(which):
        return remote(
            (u32, v32)[which], relay.at[which], relay_send.at[which], relay_recv.at[which], (relay_row, relay_col)
        )

    def onward_copy(which, slot):
        return remote(
            relay.at[which], tiles.at[slot, which], tiles_send.at[which], tiles_recv.at[slot, which],
            solver_of(from_row, n),
        )

    def inner_copy():
        return remote(own_inner, inner_second, inner_send, inner_recv, solver)

    def y_copy(slot, source, step):
        return remote(result.at[slot], arrived, y_send.at[slot, step], y_recv, (source + step, source))

    def extra_copy(slot, source):
        return remote(result.at[slot], arrived2, extra_send.at[slot], extra_recv, extra_target(source))

    def part_copy(owner, half):
        return remote(own_part, parts.at[half, owner], part_send.at[0], part_recv.at[half, owner], solver)

    def low_part_copy(owner):
        return remote(low_part, parts.at[0, owner], part_send.at[1], part_recv.at[0, owner], solver)

    def log_copy(owner, half):
        return remote(logs, logs_parts.at[half, owner], log_send, log_recv.at[half, owner], solver)

    def final_copy(slot, source, target):
        return remote(result.at[slot], final, final_send.at[slot, target], final_recv, (source, target))

    def logs_copy(slot, source, target):
        return remote(logs_all.at[slot], logs_in, logs_send.at[slot, target], logs_recv, (source, target))

    def inner_of(y, v):
        return lax.dot_general(y.astype(bf16), v, (((1,), (1,)), ((), ())), preferred_element_type=f32)

    def finish(y, log_mean):
        lik_ref[...] = log_mean
        white_ref[...] = y

    def update(inner, depth):
        result[0] = solved[0] - jnp.dot(inner, folded[pl.ds(0, depth), :], preferred_element_type=f32)

    def others(source):
        for target in range(n):
            yield target, jnp.logical_not((source == row) & (col == target))

    def share_logs(slot, source, half):
        logs_all[slot] = jnp.where(source == row, logs[...], 0.0)
        for owner, other in others(source):
            @pl.when(other)
            def _():
                log_copy(owner, half).wait_recv()
                logs_all[slot] = logs_all[slot] + logs_parts[half, owner]
        for target, other in others(source):
            @pl.when(other)
            def _():
                logs_copy(slot, source, target).start()

    def upper(half, left, right):
        return whole16[half, pl.ds(left * TILE, TILE), pl.ds(right * TILE, TILE)]

    def times_upper(lhs, half, right):
        value = jnp.zeros((lhs.shape[0], TILE), f32)
        for left in range(right + 1):
            value = value + jnp.dot(
                lhs[:, left * TILE:(left + 1) * TILE], upper(half, left, right), preferred_element_type=f32
            )
        return value

    def fold(factor, half, into, at):
        for right in range(width // TILE):
            into[pl.ds(at, rank_max), pl.ds(right * TILE, TILE)] = times_upper(factor, half, right).astype(bf16)

    def solve_far(slot, source, half, right_side, needed):
        solved[slot] = right_side
        for owner in range(n - 2):
            @pl.when(needed(owner))
            def _():
                part_copy(owner, half).wait_recv()
                solved[slot] = solved[slot] - parts[half, owner]
        reduced = solved[slot].astype(bf16)
        for right in range(width // TILE):
            solved[slot, :, pl.ds(right * TILE, TILE)] = times_upper(reduced, half, right)

    def take_block(owner, half, own):
        first = block_first(owner)
        rows = pl.ds(owner * piece, piece)
        columns = pl.ds(first, width - first)
        @pl.when(jnp.logical_not(own & (col == owner)))
        def _():
            block_copy(owner, half).wait_recv()
            whole16[half, rows, columns] = whole[half, rows, columns].astype(bf16)
        @pl.when(own & (col == owner))
        def _():
            whole16[half, rows, columns] = inv_ref[:, columns]

    def onward_copy_in(slot, which):
        return remote(relay.at[which], tiles.at[slot, which], tiles_send.at[which], tiles_recv.at[slot, which], solver)

    def send_y(slot, source, without=0):
        for step in range(1, n):
            if step == without:
                continue
            @pl.when(feeds(source, source + step))
            def _():
                y_copy(slot, source, step).start()

    def send_final(slot, source):
        for target, other in others(source):
            @pl.when(other)
            def _():
                final_copy(slot, source, target).start()

    def transposed(value):
        return value.astype(f32).T.astype(bf16)

    @pl.when(first_row & jnp.logical_not(in_row))
    def _():
        part_copy(col, parity).start()
    for owner in range(n):
        @pl.when((col == owner) & jnp.logical_not(first_row | in_row))
        def _():
            block_copy(owner, parity).start()
    @pl.when(by_relay)
    def _():
        for which in range(2):
            relay_copy(which).start()
    @pl.when(moved)
    def _():
        rs_copy().start()
        v_copy().start()
        u_copy().start()
    @pl.when(lent)
    def _():
        v_copy().start()
        u_copy().start()
    @pl.when(second)
    def _():
        second_copy().start()
    @pl.when(jnp.logical_not(in_row))
    def _():
        log_copy(col, parity).start()
    @pl.when(is_relay)
    def _():
        for which in range(2):
            relay_copy(which).wait_recv()
            onward_copy(which, onto_slot).start()

    @pl.when(is_single)
    def _():
        @pl.when(for_first)
        def _():
            y = own_part[...]
            for owner in range(1, n):
                part_copy(owner, 0).wait_recv()
                y = y + parts[0, owner]
            result[0] = y

        @pl.when(jnp.logical_not(for_first))
        def _():
            @pl.when(for_even)
            def _():
                rs_copy().wait_recv()
                v_copy().wait_recv()
                u_copy().wait_recv()
                u16[...] = u_near[...].astype(bf16)
                v_pair[:, pl.ds(0, rank_max)] = transposed(v_near[...])
                v_pair[:, pl.ds(rank_max, rank_max)] = transposed(v_ref[...])
            @pl.when(for_odd)
            def _():
                rs_near[...] = rs_ref[...]
                v_pair[:, pl.ds(0, rank_max)] = transposed(v_ref[...])
            lhs[pl.ds(0, rank_max), :] = u16[...]
            lhs[pl.ds(rank_max, 16), :] = jnp.concatenate([rs_near[...]] * (16 // nrhs), axis=0).astype(bf16)
            for left in range(width // TILE):
                for owner in range(left * TILE // piece, (left + 1) * TILE // piece):
                    take_block(owner, kind, in_row)
                for right in range(left, width // TILE):
                    value = jnp.dot(lhs[:, pl.ds(left * TILE, TILE)], upper(kind, left, right), preferred_element_type=f32)
                    columns = pl.ds(right * TILE, TILE)
                    if left:
                        value = value + products[:, columns]
                    products[:, columns] = value
            folded[pl.ds(0, rank_max), :] = products[pl.ds(0, rank_max), :].astype(bf16)
            @pl.when(mine >= SECOND)
            def _():
                second_copy().wait_recv()
                u16[...] = u_second[...].astype(bf16)
                fold(u16, kind, folded, rank_max)

            @pl.when(mine == 1)
            def _():
                solved[0] = products[pl.ds(rank_max, nrhs), :]
            @pl.when(mine > 1)
            def _():
                share_logs(0, mine, kind)
                solve_far(0, mine, kind, rs_near[...],
                          lambda owner: (owner < mine - 2) | ((owner < mine - 1) & (mine < SECOND)))

            two = mine >= SECOND
            @pl.when(for_odd & jnp.logical_not(two))
            def _():
                y_copy(0, mine, 0).wait_recv()
                inner = jnp.dot(arrived[...].astype(bf16), v_pair[:, pl.ds(0, rank_max)], preferred_element_type=f32)
                update(inner.astype(bf16), rank_max)
            @pl.when(for_even & jnp.logical_not(two))
            def _():
                y_copy(0, mine, 0).wait_recv()
                inner = jnp.dot(arrived[...].astype(bf16), v_pair[...], preferred_element_type=f32)
                own_inner[...] = inner[:, rank_max:]
                update(inner[:, :rank_max].astype(bf16), rank_max)
            @pl.when(for_odd & two)
            def _():
                y_copy(0, mine, 0).wait_recv()
                inner_copy().wait_recv()
                inner = jnp.dot(arrived[...].astype(bf16), v_pair[:, pl.ds(0, rank_max)], preferred_element_type=f32)
                update(jnp.concatenate([inner, inner_second[...]], axis=1).astype(bf16), 2 * rank_max)
            @pl.when(for_even & two)
            def _():
                y_copy(0, mine, 0).wait_recv()
                inner = jnp.dot(arrived[...].astype(bf16), v_pair[...], preferred_element_type=f32)
                own_inner[...] = inner[:, rank_max:]
                inner_copy().start()
                inner_copy().wait_recv()
                update(jnp.concatenate([inner[:, :rank_max], inner_second[...]], axis=1).astype(bf16), 2 * rank_max)

        @pl.when(feeds_extra(mine))
        def _():
            extra_copy(0, mine).start()
        send_y(0, mine)
        send_final(0, mine)
        @pl.when(for_even & sends_part)
        def _():
            own_part[...] = jnp.dot(own_inner[...].astype(bf16), u32[...].astype(bf16), preferred_element_type=f32)
            part_copy(col, parity).start()
        @pl.when(mine <= 1)
        def _():
            share_logs(0, mine, kind)

    @pl.when(pair)
    def _():
        lower, upper_row = row - 1, row
        rs_copy().wait_recv()
        v_copy().wait_recv()
        v_pair[:, pl.ds(0, rank_max)] = transposed(v_near[...])
        v_pair[:, pl.ds(rank_max, rank_max)] = transposed(v_ref[...])
        u_copy().wait_recv()
        factors[pl.ds(0, rank_max), :] = u_near[...].astype(bf16)
        factors[pl.ds(2 * rank_max, rank_max), :] = u16[...]
        for slot in range(3):
            for which in range(2):
                onward_copy_in(slot, which).wait_recv()
        factors[pl.ds(rank_max, rank_max), :] = tiles[1, 0].astype(bf16)
        factors[pl.ds(3 * rank_max, rank_max), :] = tiles[2, 0].astype(bf16)
        factors[pl.ds(4 * rank_max, rank_max), :] = tiles[0, 0].astype(bf16)
        v_pair2[:, pl.ds(0, rank_max)] = transposed(tiles[1, 1])
        v_pair2[:, pl.ds(rank_max, rank_max)] = transposed(tiles[2, 1])
        v_last[...] = transposed(tiles[0, 1])
        for left in reversed(range(width // TILE)):
            for half, at in ((0, pl.ds(0, 2 * rank_max)), (1, pl.ds(2 * rank_max, 3 * rank_max))):
                for owner in reversed(range(left * TILE // piece, (left + 1) * TILE // piece)):
                    take_block(owner, half, half == 1)
                for right in range(left, width // TILE):
                    columns = pl.ds(right * TILE, TILE)
                    value = jnp.dot(
                        factors[at, pl.ds(left * TILE, TILE)], upper(half, left, right), preferred_element_type=f32
                    )
                    if left < right:
                        value = value + sums[at, columns]
                    if left:
                        sums[at, columns] = value
                    elif half == 0:
                        folded[:, columns] = value.astype(bf16)
                    else:
                        folded2[:, columns] = value.astype(bf16)
        share_logs(0, lower, 0)
        share_logs(1, upper_row, 1)
        solved[0] = rs_near[...]
        solved[1] = rs_ref[...]
        for owner in range(n - 2):
            @pl.when(owner <= row - 6)
            def _():
                for half in range(2):
                    part_copy(owner, half).wait_recv()
                    solved[half] = solved[half] - parts[half, owner]
        own_part_of = pl.ds(0, rank_max)
        other_part_of = pl.ds(rank_max, rank_max)

        def near_products(y, v, part, first):
            inner = jnp.dot(y.astype(bf16), v, preferred_element_type=f32).astype(bf16)
            low = jnp.dot(inner[:, :rank_max], folded[part, :], preferred_element_type=f32)
            high = jnp.dot(inner[:, rank_max:], folded2[part, :], preferred_element_type=f32)
            held[0] = low if first else held[0] + low
            held[1] = high if first else held[1] + high

        @pl.when(lean(lower, n) == 1)
        def _():
            extra_copy(0, 0).wait_recv()
            near_products(arrived2[...], v_pair2[...], other_part_of, True)
            y_copy(0, mine, 0).wait_recv()
            near_products(arrived[...], v_pair[...], own_part_of, False)
        @pl.when(lean(lower, n) == 2)
        def _():
            y_copy(0, mine, 0).wait_recv()
            near_products(arrived[...], v_pair[...], own_part_of, True)
            extra_copy(0, 0).wait_recv()
            near_products(arrived2[...], v_pair2[...], other_part_of, False)
        for owner in (row - 5, row - 4):
            @pl.when(owner >= 0)
            def _():
                for half in range(2):
                    part_copy(owner, half).wait_recv()
                    solved[half] = solved[half] - parts[half, owner]
        reduced = solved[0].astype(bf16)
        y_low = jnp.concatenate(
            [times_upper(reduced, 0, right) for right in range(width // TILE)], axis=1
        ) - held[0]
        result[0] = y_low
        @pl.when(feeds_extra(lower))
        def _():
            extra_copy(0, lower).start()
        @pl.when(feeds(lower, lower + 3))
        def _():
            y_copy(0, lower, 3).start()
        last = jnp.dot(y_low.astype(bf16), v_last[...], preferred_element_type=f32).astype(bf16)
        reduced = solved[1].astype(bf16)
        result[1] = (
            jnp.concatenate([times_upper(reduced, 1, right) for right in range(width // TILE)], axis=1)
            - held[1]
            - jnp.dot(last, folded2[pl.ds(2 * rank_max, rank_max), :], preferred_element_type=f32)
        )
        @pl.when(feeds_extra(upper_row))
        def _():
            extra_copy(1, upper_row).start()
        send_y(1, upper_row)
        send_y(0, lower, without=3)
        send_final(1, upper_row)
        send_final(0, lower)

    @pl.when(double)
    def _():
        v_copy().wait_recv()
        v_pair[:, pl.ds(0, rank_max)] = transposed(v_near[...])
        v_pair[:, pl.ds(rank_max, rank_max)] = transposed(v_ref[...])
        u_copy().wait_recv()
        folded[pl.ds(0, rank_max), :] = u_near[...].astype(bf16)
        y_copy(0, mine, 0).wait_recv()
        inner = jnp.dot(arrived[...].astype(bf16), v_pair[...], preferred_element_type=f32).astype(bf16)
        low_part[...] = jnp.dot(inner[:, :rank_max], folded[pl.ds(0, rank_max), :], preferred_element_type=f32)
        own_part[...] = jnp.dot(inner[:, rank_max:], u16[...], preferred_element_type=f32)
        low_part_copy(col).start()
        part_copy(col, 1).start()

    @pl.when(is_worker)
    def _():
        y_copy(0, mine, 0).wait_recv()
        inner = inner_of(arrived[...], v_ref[...])
        @pl.when(second)
        def _():
            own_inner[...] = inner
            inner_copy().start()
        @pl.when(sends_part)
        def _():
            own_part[...] = jnp.dot(inner.astype(bf16), u16[...], preferred_element_type=f32)
            part_copy(col, parity).start()

    @pl.when(pair)
    def _():
        finish(result[1], logs_all[1])
    @pl.when(in_row & jnp.logical_not(pair))
    def _():
        finish(result[0], logs_all[0])
    @pl.when(jnp.logical_not(in_row))
    def _():
        logs_copy(0, mine, 0).wait_recv()
        final_copy(0, mine, 0).wait_recv()
        finish(final[...], logs_in[...])

    for owner in range(n):
        @pl.when((col == owner) & jnp.logical_not(first_row | in_row))
        def _():
            block_copy(owner, parity).wait_send()
    @pl.when(moved)
    def _():
        rs_copy().wait_send()
        v_copy().wait_send()
        u_copy().wait_send()
    @pl.when(lent)
    def _():
        v_copy().wait_send()
        u_copy().wait_send()
    @pl.when(double)
    def _():
        low_part_copy(col).wait_send()
        part_copy(col, 1).wait_send()
    @pl.when(second)
    def _():
        second_copy().wait_send()
        inner_copy().wait_send()
    @pl.when(by_relay)
    def _():
        for which in range(2):
            relay_copy(which).wait_send()
    @pl.when(is_relay)
    def _():
        for which in range(2):
            onward_copy(which, onto_slot).wait_send()
    @pl.when(jnp.logical_not(in_row))
    def _():
        log_copy(col, parity).wait_send()
    @pl.when(sends_part | (first_row & jnp.logical_not(in_row)))
    def _():
        part_copy(col, parity).wait_send()
    for slot, source, active in served:
        @pl.when(active)
        def _():
            @pl.when(feeds_extra(source))
            def _():
                extra_copy(slot, source).wait_send()
            for step in range(1, n):
                @pl.when(feeds(source, source + step))
                def _():
                    y_copy(slot, source, step).wait_send()
            for target, other in others(source):
                @pl.when(other)
                def _():
                    final_copy(slot, source, target).wait_send()
                    logs_copy(slot, source, target).wait_send()


def outputs(y_ref, log_ref, white_ref, lik_ref):
    y = y_ref[...]
    nrhs, width = y.shape
    lik = -0.5 * jnp.sum(y * y, axis=1, keepdims=True) * (1.0 / width) + log_ref[0:1, 0:1] - 0.5 * math.log(2.0 * math.pi)
    diagonal = lax.broadcasted_iota(jnp.int32, (nrhs, nrhs), 0) == lax.broadcasted_iota(jnp.int32, (nrhs, nrhs), 1)
    lik_ref[...] = jnp.sum(jnp.where(diagonal, lik, 0.0), axis=0, keepdims=True)
    white_ref[...] = y


def local(n, right_side, inverse_t, u_factor, v_factor, ranks):
    nrhs, width = right_side.shape[2:]
    piece = inverse_t.shape[2]
    rank_max = u_factor.shape[4]
    f32, bf16 = jnp.float32, jnp.bfloat16
    vmem = pl.BlockSpec(memory_space=pltpu.VMEM)
    dma = pltpu.SemaphoreType.DMA
    rows = pltpu.VMEM((nrhs, width), f32)
    two_rows = pltpu.VMEM((2, nrhs, width), f32)
    small = pltpu.VMEM((8, LANES), f32)
    factor32 = pltpu.VMEM((rank_max, width), f32)
    factor16 = pltpu.VMEM((rank_max, width), bf16)
    inner = pltpu.VMEM((nrhs, rank_max), f32)
    y, log_mean = pl.pallas_call(
        functools.partial(kernel, n),
        out_shape=(jax.ShapeDtypeStruct((nrhs, width), f32), jax.ShapeDtypeStruct((8, LANES), f32)),
        in_specs=[vmem, vmem, vmem, vmem, pl.BlockSpec(memory_space=pltpu.SMEM)],
        out_specs=(vmem, vmem),
        scratch_shapes=[
            pltpu.VMEM((piece, width), f32),
            pltpu.VMEM((2, width, width), f32),
            pltpu.VMEM((2, width, width), bf16),
            factor32,
            factor32,
            factor16,
            factor32,
            factor32,
            pltpu.VMEM((width, 2 * rank_max), bf16),
            pltpu.VMEM((width, 2 * rank_max), bf16),
            pltpu.VMEM((width, rank_max), bf16),
            pltpu.VMEM((5 * rank_max, width), bf16),
            pltpu.VMEM((5 * rank_max, width), f32),
            factor32,
            rows,
            pltpu.VMEM((3, 2, rank_max, width), f32),
            pltpu.VMEM((2, rank_max, width), f32),
            pltpu.VMEM((2 * rank_max, width), bf16),
            pltpu.VMEM((3 * rank_max, width), bf16),
            pltpu.VMEM((max(piece, LANES), width), bf16),
            pltpu.VMEM((rank_max + 16, width), bf16),
            pltpu.VMEM((rank_max + 16, width), f32),
            rows,
            rows,
            rows,
            rows,
            pltpu.VMEM((2, n, nrhs, width), f32),
            inner,
            inner,
            two_rows,
            two_rows,
            two_rows,
            rows,
            small,
            pltpu.VMEM((2, n, 8, LANES), f32),
            pltpu.VMEM((2, 8, LANES), f32),
            small,
            dma, dma((2, n)), dma((4,)), dma((4,)), dma, dma, dma((2, n)), dma, dma((2,)), dma,
            dma((2,)), dma((2, n)), dma((2, n)), dma, dma, dma((2, n)), dma((2, n)), dma,
            dma((2,)), dma((2,)), dma((2,)), dma((3, 2)),
        ],
        compiler_params=pltpu.CompilerParams(collective_id=0, has_side_effects=True),
    )(
        right_side.reshape(nrhs, width),
        inverse_t.reshape(piece, width),
        u_factor.reshape(rank_max, width),
        v_factor.reshape(rank_max, width),
        ranks.reshape(1, 1),
    )
    white, lik = pl.pallas_call(
        outputs,
        out_shape=(jax.ShapeDtypeStruct((nrhs, width), f32), jax.ShapeDtypeStruct((1, nrhs), f32)),
        in_specs=[vmem, vmem],
        out_specs=(vmem, vmem),
    )(y, log_mean)
    return white.reshape(1, 1, nrhs, width), lik.reshape(1, 1, nrhs)


def solution(mesh):
    return jax.shard_map(
        functools.partial(local, mesh.shape["row"]),
        mesh=mesh,
        in_specs=(
            P(None, "row", None, None),
            P(None, "row", "col", None),
            P(None, "row", None, "col", None, None),
            P(None, "row", None, "col", None, None),
            P(None, "row", None, "col"),
        ),
        out_specs=(P(None, "row", None, None), P(None, "row", None)),
        check_vma=False,
    )
```

time: 65.9 us -> 61.6 us (0.935); the launches traced: 65.7 us -> 60.4 us
  Pallas kernels: 64.4 us -> 59.1 us
    pallas_call x1, Pallas kernels: 63 us -> 57.7 us  [local(): pl.pallas_call(functools.partial(kernel, n), out_shape=(jax.ShapeDtypeStr...]
where the time goes in v5:
time: 61.6 us; the launch traced here: 60.4 us
  Pallas kernels  59.1 us (96%)
  between operations  1.29 us (2%)
    pallas_call x1, Pallas kernels, local(): pl.pallas_call(functools.partial(kernel, n), out_shape=(jax.ShapeDtypeStr...  57.7 us
    pallas_call x1, Pallas kernels, local(): pl.pallas_call(outputs, out_shape=(jax.ShapeDtypeStruct((nrhs, width), f3...  1.4 us

profile of v5, /device:TPU:225, one launch (start us, length us, event | category | flops | bytes accessed | tf_op | source)
XLA Modules:
  0.0 60.4 jit_solution(11628828327719117335)
XLA Ops:
  1.3 57.7 %shard_map.68 = (f32[4,1024]{1,0:T(4,128)}, f32[8,128]{1,0:T(8,128)}) custom-call(f32[4,1024]{1,0:T(4,128)} %bitcast.11, bf16[64,1024]{1,0:T(8,128)(2,1)} %bitcast.10, bf16[128,1024]{1,0:T(8,128)(2,1)} %bitcast.8, bf16[128,1024]{1,0:T(8,128)(2,1)} %bitcast.9, s32[1,1]{1,0:T(1,128)} %bitcast.7.rank_ref), custom_call_target="tpu_custom_call" | custom-call | tf_op jit(solution)/shard_map/pallas_call | solution.py:677
  59.0 1.4 %shard_map.69 = (f32[4,1024]{1,0:T(4,128)}, f32[1,4]{1,0:T(1,128)}) custom-call(f32[4,1024]{1,0:T(4,128)} %get-tuple-element.6.y_ref, f32[8,128]{1,0:T(8,128)} %get-tuple-element.7.log_ref), custom_call_target="tpu_custom_call" | custom-call | tf_op jit(solution)/shard_map/pallas_call | solution.py:732

commit v6 on v5

--- a/solution.py
+++ b/solution.py
@@ -15,7 +15,7 @@
 
 
 def first_pair(n):
-    return 10 if n == 16 else 2
+    return 6 if n == 16 else 2
 
 
 def lean(base, n):
@@ -34,13 +34,13 @@
 
 
 def kernel(n, rs_ref, inv_ref, u_ref, v_ref, rank_ref, white_ref, lik_ref,
-           block, whole, whole16, u32, v32, u16, u_near, v_near, v_pair, v_pair2, v_last, factors, sums, u_second, rs_near,
+           block, block_in, whole, whole16, u32, v32, u16, u_near, v_near, v_pair, v_pair2, v_last, factors, sums, u_second, rs_near,
            tiles, relay, folded, folded2, padded, lhs, products,
            arrived, arrived2, own_part, low_part, parts, own_inner, inner_second, held, solved, result, final,
            logs, logs_parts, logs_all, logs_in,
            block_send, block_recv, tile_send, tile_recv, inner_send, inner_recv, y_send, y_recv, extra_send, extra_recv,
            part_send, part_recv, final_send, final_recv, log_send, log_recv, logs_send, logs_recv,
-           relay_send, relay_recv, tiles_send, tiles_recv):
+           relay_send, relay_recv, tiles_send, tiles_recv, detour_send, detour_recv):
     row = lax.axis_index("row")
     col = lax.axis_index("col")
     piece, width = inv_ref.shape
@@ -82,18 +82,44 @@
     takes_y = jnp.where(paired, double | pair, (col < row) & jnp.logical_not(moved))
     sends_part = single & ((col < row - 2) | ((col == row - 2) & (row < SECOND)))
     is_worker = takes_y & single & jnp.logical_not(is_solver)
-    relay_row = jnp.where(by_x, row, jnp.where(by_up, lax.rem(row + 2, n), row - 2))
-    relay_col = jnp.where(by_x, lax.rem(own_col + shift, n), own_col)
-    up_row = lax.rem(row + n - 2, n)
+    west_row, west_col = (row, lax.rem(own_col + n - shift, n)) if n == 16 else (row - 2, own_col)
+    def goes_up(base):
+        return (lean(base, n) == 2) | (base > start_pairs)
+
+    z_row = jnp.where(goes_up(pair_row), lax.rem(row + 2, n), row - 2)
+    relay_row = jnp.where(by_x, row, jnp.where(by_up, z_row, west_row))
+    relay_col = jnp.where(by_x, lax.rem(own_col + shift, n), jnp.where(by_up, own_col, west_col))
     x_relay = paired & odd & (col == lax.rem(own_col + shift, n))
-    up_relay = jnp.logical_not(odd) & (up_row >= start_pairs) & (col == up_row - lean(up_row, n))
-    down_relay = odd & (row + 2 > start_pairs) & (row + 2 < n) & (col == row + 1 - lean(row + 1, n))
-    is_relay = x_relay | up_relay | down_relay
-    from_row = jnp.where(x_relay, row, jnp.where(up_relay, up_row, row + 2))
+    below_row, above_row = lax.rem(row + n - 2, n), row + 2
+    from_below = (below_row >= start_pairs) & goes_up(below_row) & (col == below_row - lean(below_row, n))
+    from_above = (
+        (above_row < n) & (above_row >= start_pairs) & jnp.logical_not(goes_up(above_row)) & (col == above_row - 1)
+    )
+    up_relay = jnp.logical_not(odd) & (from_below | from_above)
+    up_row = jnp.where(from_below, below_row, above_row)
+    if n == 16:
+        west_relay = paired & odd & (col == west_col)
+        west_from = row
+    else:
+        west_relay = odd & (row + 2 > start_pairs) & (row + 2 < n) & (col == row + 1 - lean(row + 1, n))
+        west_from = row + 2
+    is_relay = x_relay | up_relay | west_relay
+    from_row = jnp.where(x_relay, row, jnp.where(up_relay, up_row, west_from))
     from_col = jnp.where(
-        x_relay, row - 1, jnp.where(up_relay, up_row - 3 + lean(up_row, n), row - 2 + lean(row + 1, n))
+        x_relay, row - 1,
+        jnp.where(up_relay, up_row - 3 + lean(up_row, n), west_from - 4 + lean(west_from - 1, n))
     )
     onto_slot = jnp.where(x_relay, 0, jnp.where(up_relay, 1, 2))
+
+    detours = [(2, 1, row == 1)]
+    if n == 16:
+        detours += [(0, 3, paired & (lean(pair_row, n) == 2)), (4, 7, paired & (lean(pair_row, n) == 2))]
+    takes_detour, detour_col, serves_detour, detour_from = False, 0, False, 0
+    for owner, third, condition in detours:
+        takes_detour = takes_detour | (condition & (col == owner))
+        detour_col = jnp.where(col == owner, third, detour_col)
+        serves_detour = serves_detour | (condition & (col == third))
+        detour_from = jnp.where(col == third, owner, detour_from)
 
     def feeds(source, target):
         base = target - lax.rem(target, 2)
@@ -135,6 +161,10 @@
         waits = waits + jnp.where(active, met, 0)
     waits = waits + greet(jnp.logical_not(in_row), solver)
     waits = waits + greet(takes_y, solver_of(col, n))
+    greet(takes_detour, (row, detour_col))
+    greet(serves_detour, (row, detour_from))
+    waits = waits + takes_detour.astype(jnp.int32) + serves_detour.astype(jnp.int32)
+
     @pl.when(paired)
     def _():
         greet(pair, solver_of(other_col, n))
@@ -142,8 +172,8 @@
         greet(lent, (row + 1, col))
         greet(double, (row - 1, col))
         greet(pair, (row, lax.rem(own_col + shift, n)))
-        greet(pair, (lax.rem(row + 1, n), col))
-        greet(pair, (row - 2, col))
+        greet(pair, (jnp.where(goes_up(pair_row), lax.rem(row + 1, n), row - 3), col))
+        greet(pair, (west_row, west_col))
     @pl.when(is_relay)
     def _():
         greet(is_relay, (from_row, from_col))
@@ -207,6 +237,17 @@
 
     tile_device = (jnp.where(lent, row + 1, solver[0]), jnp.where(lent, col, solver[1]))
 
+    def detour_copy():
+        return remote(block, block_in, block_send, detour_recv, (row, detour_col))
+
+    def detour_onward(owner):
+        first = block_first(owner)
+        return remote(
+            block_in.at[:, pl.ds(first, width - first)],
+            whole.at[parity, pl.ds(owner * piece, piece), pl.ds(first, width - first)],
+            detour_send, block_recv.at[parity, owner], solver,
+        )
+
     def u_copy():
         return remote(u32, u_near, tile_send.at[0], tile_recv.at[0], tile_device)
 
@@ -342,9 +383,12 @@
     def _():
         part_copy(col, parity).start()
     for owner in range(n):
-        @pl.when((col == owner) & jnp.logical_not(first_row | in_row))
+        @pl.when((col == owner) & jnp.logical_not(first_row | in_row | takes_detour))
         def _():
             block_copy(owner, parity).start()
+    @pl.when(takes_detour)
+    def _():
+        detour_copy().start()
     @pl.when(by_relay)
     def _():
         for which in range(2):
@@ -364,6 +408,11 @@
     @pl.when(jnp.logical_not(in_row))
     def _():
         log_copy(col, parity).start()
+    for owner, third, condition in detours:
+        @pl.when(condition & (col == third))
+        def _():
+            detour_copy().wait_recv()
+            detour_onward(owner).start()
     @pl.when(is_relay)
     def _():
         for which in range(2):
@@ -601,9 +650,16 @@
         finish(final[...], logs_in[...])
 
     for owner in range(n):
-        @pl.when((col == owner) & jnp.logical_not(first_row | in_row))
+        @pl.when((col == owner) & jnp.logical_not(first_row | in_row | takes_detour))
         def _():
             block_copy(owner, parity).wait_send()
+    @pl.when(takes_detour)
+    def _():
+        detour_copy().wait_send()
+    for owner, third, condition in detours:
+        @pl.when(condition & (col == third))
+        def _():
+            detour_onward(owner).wait_send()
     @pl.when(moved)
     def _():
         rs_copy().wait_send()
@@ -680,6 +736,7 @@
         in_specs=[vmem, vmem, vmem, vmem, pl.BlockSpec(memory_space=pltpu.SMEM)],
         out_specs=(vmem, vmem),
         scratch_shapes=[
+            pltpu.VMEM((piece, width), f32),
             pltpu.VMEM((piece, width), f32),
             pltpu.VMEM((2, width, width), f32),
             pltpu.VMEM((2, width, width), bf16),
@@ -719,7 +776,7 @@
             small,
             dma, dma((2, n)), dma((4,)), dma((4,)), dma, dma, dma((2, n)), dma, dma((2,)), dma,
             dma((2,)), dma((2, n)), dma((2, n)), dma, dma, dma((2, n)), dma((2, n)), dma,
-            dma((2,)), dma((2,)), dma((2,)), dma((3, 2)),
+            dma((2,)), dma((2,)), dma((2,)), dma((3, 2)), dma, dma,
         ],
         compiler_params=pltpu.CompilerParams(collective_id=0, has_side_effects=True),
     )(

time: 61.6 us -> 58.2 us (0.945)
  the two profiles are of different devices: /device:TPU:225 before, /device:TPU:250 now
where the time goes in v6:
time: 58.2 us; the launch traced here: 58 us
  Pallas kernels  56.7 us (97%)
  between operations  1.29 us (2%)
    pallas_call x1, Pallas kernels, local(): pl.pallas_call(functools.partial(kernel, n), out_shape=(jax.ShapeDtypeStr...  55.3 us
    pallas_call x1, Pallas kernels, local(): pl.pallas_call(outputs, out_shape=(jax.ShapeDtypeStruct((nrhs, width), f3...  1.4 us

profile of v6, /device:TPU:250, one launch (start us, length us, event | category | flops | bytes accessed | tf_op | source)
XLA Modules:
  0.0 58.0 jit_solution(8698942001404466039)
XLA Ops:
  1.3 55.3 %shard_map.68 = (f32[4,1024]{1,0:T(4,128)}, f32[8,128]{1,0:T(8,128)}) custom-call(f32[4,1024]{1,0:T(4,128)} %bitcast.11, bf16[64,1024]{1,0:T(8,128)(2,1)} %bitcast.10, bf16[128,1024]{1,0:T(8,128)(2,1)} %bitcast.8, bf16[128,1024]{1,0:T(8,128)(2,1)} %bitcast.9, s32[1,1]{1,0:T(1,128)} %bitcast.7.rank_ref), custom_call_target="tpu_custom_call" | custom-call | tf_op jit(solution)/shard_map/pallas_call | solution.py:733
  56.6 1.4 %shard_map.69 = (f32[4,1024]{1,0:T(4,128)}, f32[1,4]{1,0:T(1,128)}) custom-call(f32[4,1024]{1,0:T(4,128)} %get-tuple-element.6.y_ref, f32[8,128]{1,0:T(8,128)} %get-tuple-element.7.log_ref), custom_call_target="tpu_custom_call" | custom-call | tf_op jit(solution)/shard_map/pallas_call | solution.py:789

commit v7 on v6

--- a/solution.py
+++ b/solution.py
@@ -111,15 +111,23 @@
     )
     onto_slot = jnp.where(x_relay, 0, jnp.where(up_relay, 1, 2))
 
-    detours = [(2, 1, row == 1)]
+    even_out = paired & (lean(pair_row, n) == 2)
     if n == 16:
-        detours += [(0, 3, paired & (lean(pair_row, n) == 2)), (4, 7, paired & (lean(pair_row, n) == 2))]
-    takes_detour, detour_col, serves_detour, detour_from = False, 0, False, 0
-    for owner, third, condition in detours:
-        takes_detour = takes_detour | (condition & (col == owner))
-        detour_col = jnp.where(col == owner, third, detour_col)
-        serves_detour = serves_detour | (condition & (col == third))
-        detour_from = jnp.where(col == third, owner, detour_from)
+        detours = [
+            (6, 4, 0, row == 1), (7, 4, 1, row == 1),
+            (4, 5, 0, row == 2), (6, 5, 1, row == 2),
+            (4, 6, 0, row == 3), (5, 6, 1, row == 3),
+            (0, 3, 0, even_out), (4, 7, 0, even_out),
+            (7, 4, 0, pair_row == start_pairs),
+        ]
+    else:
+        detours = [(2, 1, 0, row == 1), (3, 1, 1, row == 1)]
+    takes_detour, detour_col, detour_slot = False, 0, 0
+    for owner, third, slot, condition in detours:
+        takes = condition & (col == owner)
+        takes_detour = takes_detour | takes
+        detour_col = jnp.where(takes, third, detour_col)
+        detour_slot = jnp.where(takes, slot, detour_slot)
 
     def feeds(source, target):
         base = target - lax.rem(target, 2)
@@ -162,8 +170,9 @@
     waits = waits + greet(jnp.logical_not(in_row), solver)
     waits = waits + greet(takes_y, solver_of(col, n))
     greet(takes_detour, (row, detour_col))
-    greet(serves_detour, (row, detour_from))
-    waits = waits + takes_detour.astype(jnp.int32) + serves_detour.astype(jnp.int32)
+    waits = waits + takes_detour.astype(jnp.int32)
+    for owner, third, slot, condition in detours:
+        waits = waits + greet(condition & (col == third), (row, owner))
 
     @pl.when(paired)
     def _():
@@ -237,15 +246,15 @@
 
     tile_device = (jnp.where(lent, row + 1, solver[0]), jnp.where(lent, col, solver[1]))
 
-    def detour_copy():
-        return remote(block, block_in, block_send, detour_recv, (row, detour_col))
-
-    def detour_onward(owner):
+    def detour_copy(slot):
+        return remote(block, block_in.at[slot], block_send, detour_recv.at[slot], (row, detour_col))
+
+    def detour_onward(owner, slot):
         first = block_first(owner)
         return remote(
-            block_in.at[:, pl.ds(first, width - first)],
+            block_in.at[slot, :, pl.ds(first, width - first)],
             whole.at[parity, pl.ds(owner * piece, piece), pl.ds(first, width - first)],
-            detour_send, block_recv.at[parity, owner], solver,
+            detour_send.at[slot], block_recv.at[parity, owner], solver,
         )
 
     def u_copy():
@@ -388,7 +397,7 @@
             block_copy(owner, parity).start()
     @pl.when(takes_detour)
     def _():
-        detour_copy().start()
+        detour_copy(detour_slot).start()
     @pl.when(by_relay)
     def _():
         for which in range(2):
@@ -408,11 +417,11 @@
     @pl.when(jnp.logical_not(in_row))
     def _():
         log_copy(col, parity).start()
-    for owner, third, condition in detours:
+    for owner, third, slot, condition in detours:
         @pl.when(condition & (col == third))
         def _():
-            detour_copy().wait_recv()
-            detour_onward(owner).start()
+            detour_copy(slot).wait_recv()
+            detour_onward(owner, slot).start()
     @pl.when(is_relay)
     def _():
         for which in range(2):
@@ -595,6 +604,9 @@
         @pl.when(feeds(lower, lower + 3))
         def _():
             y_copy(0, lower, 3).start()
+        @pl.when(row == n - 1)
+        def _():
+            send_final(0, lower)
         last = jnp.dot(y_low.astype(bf16), v_last[...], preferred_element_type=f32).astype(bf16)
         reduced = solved[1].astype(bf16)
         result[1] = (
@@ -608,7 +620,9 @@
         send_y(1, upper_row)
         send_y(0, lower, without=3)
         send_final(1, upper_row)
-        send_final(0, lower)
+        @pl.when(row < n - 1)
+        def _():
+            send_final(0, lower)
 
     @pl.when(double)
     def _():
@@ -620,8 +634,8 @@
         y_copy(0, mine, 0).wait_recv()
         inner = jnp.dot(arrived[...].astype(bf16), v_pair[...], preferred_element_type=f32).astype(bf16)
         low_part[...] = jnp.dot(inner[:, :rank_max], folded[pl.ds(0, rank_max), :], preferred_element_type=f32)
+        low_part_copy(col).start()
         own_part[...] = jnp.dot(inner[:, rank_max:], u16[...], preferred_element_type=f32)
-        low_part_copy(col).start()
         part_copy(col, 1).start()
 
     @pl.when(is_worker)
@@ -655,11 +669,11 @@
             block_copy(owner, parity).wait_send()
     @pl.when(takes_detour)
     def _():
-        detour_copy().wait_send()
-    for owner, third, condition in detours:
+        detour_copy(detour_slot).wait_send()
+    for owner, third, slot, condition in detours:
         @pl.when(condition & (col == third))
         def _():
-            detour_onward(owner).wait_send()
+            detour_onward(owner, slot).wait_send()
     @pl.when(moved)
     def _():
         rs_copy().wait_send()
@@ -737,7 +751,7 @@
         out_specs=(vmem, vmem),
         scratch_shapes=[
             pltpu.VMEM((piece, width), f32),
-            pltpu.VMEM((piece, width), f32),
+            pltpu.VMEM((3, piece, width), f32),
             pltpu.VMEM((2, width, width), f32),
             pltpu.VMEM((2, width, width), bf16),
             factor32,
@@ -776,7 +790,7 @@
             small,
             dma, dma((2, n)), dma((4,)), dma((4,)), dma, dma, dma((2, n)), dma, dma((2,)), dma,
             dma((2,)), dma((2, n)), dma((2, n)), dma, dma, dma((2, n)), dma((2, n)), dma,
-            dma((2,)), dma((2,)), dma((2,)), dma((3, 2)), dma, dma,
+            dma((2,)), dma((2,)), dma((2,)), dma((3, 2)), dma((3,)), dma((3,)),
         ],
         compiler_params=pltpu.CompilerParams(collective_id=0, has_side_effects=True),
     )(

time: 58.2 us -> 57 us (0.979)
  the two profiles are of different devices: /device:TPU:250 before, /device:TPU:225 now
where the time goes in v7:
time: 57 us; the launch traced here: 56.5 us
  Pallas kernels  55.2 us (97%)
  between operations  1.29 us (2%)
    pallas_call x1, Pallas kernels, local(): pl.pallas_call(functools.partial(kernel, n), out_shape=(jax.ShapeDtypeStr...  53.8 us
    pallas_call x1, Pallas kernels, local(): pl.pallas_call(outputs, out_shape=(jax.ShapeDtypeStruct((nrhs, width), f3...  1.4 us

profile of v7, /device:TPU:225, one launch (start us, length us, event | category | flops | bytes accessed | tf_op | source)
XLA Modules:
  0.0 56.5 jit_solution(15206396589895605980)
XLA Ops:
  1.3 53.8 %shard_map.68 = (f32[4,1024]{1,0:T(4,128)}, f32[8,128]{1,0:T(8,128)}) custom-call(f32[4,1024]{1,0:T(4,128)} %bitcast.11, bf16[64,1024]{1,0:T(8,128)(2,1)} %bitcast.10, bf16[128,1024]{1,0:T(8,128)(2,1)} %bitcast.8, bf16[128,1024]{1,0:T(8,128)(2,1)} %bitcast.9, s32[1,1]{1,0:T(1,128)} %bitcast.7.rank_ref), custom_call_target="tpu_custom_call" | custom-call | tf_op jit(solution)/shard_map/pallas_call | solution.py:747
  55.1 1.4 %shard_map.69 = (f32[4,1024]{1,0:T(4,128)}, f32[1,4]{1,0:T(1,128)}) custom-call(f32[4,1024]{1,0:T(4,128)} %get-tuple-element.6.y_ref, f32[8,128]{1,0:T(8,128)} %get-tuple-element.7.log_ref), custom_call_target="tpu_custom_call" | custom-call | tf_op jit(solution)/shard_map/pallas_call | solution.py:803

commit v8 on v7

--- a/solution.py
+++ b/solution.py
@@ -587,12 +587,14 @@
             near_products(arrived[...], v_pair[...], own_part_of, True)
             extra_copy(0, 0).wait_recv()
             near_products(arrived2[...], v_pair2[...], other_part_of, False)
-        for owner in (row - 5, row - 4):
-            @pl.when(owner >= 0)
-            def _():
-                for half in range(2):
+        def last_far(half):
+            for owner in (row - 5, row - 4):
+                @pl.when(owner >= 0)
+                def _():
                     part_copy(owner, half).wait_recv()
                     solved[half] = solved[half] - parts[half, owner]
+
+        last_far(0)
         reduced = solved[0].astype(bf16)
         y_low = jnp.concatenate(
             [times_upper(reduced, 0, right) for right in range(width // TILE)], axis=1
@@ -604,6 +606,7 @@
         @pl.when(feeds(lower, lower + 3))
         def _():
             y_copy(0, lower, 3).start()
+        last_far(1)
         @pl.when(row == n - 1)
         def _():
             send_final(0, lower)

time: 57 us -> 56.7 us (level)
  no operation moved by 1% of the time
where the time goes in v8:
time: 56.7 us; the launch traced here: 56.3 us
  Pallas kernels  55 us (97%)
  between operations  1.29 us (2%)
    pallas_call x1, Pallas kernels, local(): pl.pallas_call(functools.partial(kernel, n), out_shape=(jax.ShapeDtypeStr...  53.6 us
    pallas_call x1, Pallas kernels, local(): pl.pallas_call(outputs, out_shape=(jax.ShapeDtypeStruct((nrhs, width), f3...  1.4 us

profile of v8, /device:TPU:225, one launch (start us, length us, event | category | flops | bytes accessed | tf_op | source)
XLA Modules:
  0.0 56.3 jit_solution(9682680367136512173)
XLA Ops:
  1.3 53.6 %shard_map.68 = (f32[4,1024]{1,0:T(4,128)}, f32[8,128]{1,0:T(8,128)}) custom-call(f32[4,1024]{1,0:T(4,128)} %bitcast.11, bf16[64,1024]{1,0:T(8,128)(2,1)} %bitcast.10, bf16[128,1024]{1,0:T(8,128)(2,1)} %bitcast.8, bf16[128,1024]{1,0:T(8,128)(2,1)} %bitcast.9, s32[1,1]{1,0:T(1,128)} %bitcast.7.rank_ref), custom_call_target="tpu_custom_call" | custom-call | tf_op jit(solution)/shard_map/pallas_call | solution.py:750
  54.9 1.4 %shard_map.69 = (f32[4,1024]{1,0:T(4,128)}, f32[1,4]{1,0:T(1,128)}) custom-call(f32[4,1024]{1,0:T(4,128)} %get-tuple-element.6.y_ref, f32[8,128]{1,0:T(8,128)} %get-tuple-element.7.log_ref), custom_call_target="tpu_custom_call" | custom-call | tf_op jit(solution)/shard_map/pallas_call | solution.py:806

commit v9 on v8

--- a/solution.py
+++ b/solution.py
@@ -371,9 +371,9 @@
     def onward_copy_in(slot, which):
         return remote(relay.at[which], tiles.at[slot, which], tiles_send.at[which], tiles_recv.at[slot, which], solver)
 
-    def send_y(slot, source, without=0):
+    def send_y(slot, source, without=()):
         for step in range(1, n):
-            if step == without:
+            if step in without:
                 continue
             @pl.when(feeds(source, source + step))
             def _():
@@ -603,9 +603,10 @@
         @pl.when(feeds_extra(lower))
         def _():
             extra_copy(0, lower).start()
-        @pl.when(feeds(lower, lower + 3))
-        def _():
-            y_copy(0, lower, 3).start()
+        for step in (3, 5):
+            @pl.when(feeds(lower, lower + step))
+            def _():
+                y_copy(0, lower, step).start()
         last_far(1)
         @pl.when(row == n - 1)
         def _():
@@ -621,7 +622,7 @@
         def _():
             extra_copy(1, upper_row).start()
         send_y(1, upper_row)
-        send_y(0, lower, without=3)
+        send_y(0, lower, without=(3, 5))
         send_final(1, upper_row)
         @pl.when(row < n - 1)
         def _():

time: 56.7 us -> 56.7 us (level)
  no operation moved by 1% of the time
where the time goes in v9:
time: 56.7 us; the launch traced here: 56.2 us
  Pallas kernels  54.9 us (97%)
  between operations  1.29 us (2%)
    pallas_call x1, Pallas kernels, local(): pl.pallas_call(functools.partial(kernel, n), out_shape=(jax.ShapeDtypeStr...  53.5 us
    pallas_call x1, Pallas kernels, local(): pl.pallas_call(outputs, out_shape=(jax.ShapeDtypeStruct((nrhs, width), f3...  1.4 us

profile of v9, /device:TPU:225, one launch (start us, length us, event | category | flops | bytes accessed | tf_op | source)
XLA Modules:
  0.0 56.2 jit_solution(9725587795214802605)
XLA Ops:
  1.3 53.5 %shard_map.68 = (f32[4,1024]{1,0:T(4,128)}, f32[8,128]{1,0:T(8,128)}) custom-call(f32[4,1024]{1,0:T(4,128)} %bitcast.11, bf16[64,1024]{1,0:T(8,128)(2,1)} %bitcast.10, bf16[128,1024]{1,0:T(8,128)(2,1)} %bitcast.8, bf16[128,1024]{1,0:T(8,128)(2,1)} %bitcast.9, s32[1,1]{1,0:T(1,128)} %bitcast.7.rank_ref), custom_call_target="tpu_custom_call" | custom-call | tf_op jit(solution)/shard_map/pallas_call | solution.py:751
  54.8 1.4 %shard_map.69 = (f32[4,1024]{1,0:T(4,128)}, f32[1,4]{1,0:T(1,128)}) custom-call(f32[4,1024]{1,0:T(4,128)} %get-tuple-element.6.y_ref, f32[8,128]{1,0:T(8,128)} %get-tuple-element.7.log_ref), custom_call_target="tpu_custom_call" | custom-call | tf_op jit(solution)/shard_map/pallas_call | solution.py:807
